TPU v7x, 32 devices: a whole 2x2x4 slice. The times are simulated.
32 devices in a mesh: space: 16 (over z, y, core), lat: 2 (over x).
Axes of the slice: x: 2, y: 2, z: 4, core: 2. Of those that a mesh axis runs over, the one named last changes fastest.
Arguments:
- fields: bfloat16 [4, 64, 3, 65536], P(None, None, None, ('space', 'lat')), may hold values from -6 to 6
- cell_latent: int32 [65536], P(('space', 'lat')), may hold values from 0 to 1023, as said below
- enc_weight: float32 [3, 65536], P(None, ('space', 'lat')), may hold values from -0.4375 to 0.4375
- dec_weight: float32 [3, 65536], P(None, ('space', 'lat')), may hold values from -5 to 5
- trans_weight: bfloat16 [1024, 64, 5120], P(('space', 'lat')), may hold values from -0.15625 to 0.15625
- graph_logits: float32 [1024, 5120], P(('space', 'lat')), may hold values from -6 to 6
- hidden_bias: float32 [1024, 64], P(('space', 'lat')), may hold values from -3 to 3
- out_weight: float32 [1024, 64], P(('space', 'lat')), may hold values from -0.75 to 0.75
- noise_var: float32 [1024], P(('space', 'lat')), may hold values from 0.005 to 0.05
Outputs:
- grad_enc: float32 [3, 65536], P(None, ('space', 'lat'))
- grad_dec: float32 [3, 65536], P(None, ('space', 'lat'))
- grad_trans: bfloat16 [1024, 64, 5120], P(('space', 'lat'))
- grad_graph: float32 [1024, 5120], P(('space', 'lat'))
Inputs may be any that keep to these rules, and one draw needn't show every extreme that they name: `cell_latent`: cells d * 2048 to (d + 1) * 2048 - 1 are assigned latents from (d - 1) * 32 to (d + 2) * 32 - 1; for every d other than the first, the first of these cells has a latent below d * 32, and for every d other than the last, the last has one at (d + 1) * 32 or above.
All inputs are finite; a program needn't handle non-finite values.
Results may differ from a plain program's by a relative error of at most 0.0023.
The roundings to bfloat16 on the way count: a program that leaves them out, or rounds other values in their place, can miss the bound.
Values may be sent and summed in bfloat16 or wider, within the bound.
No kernel may reach another device: no remote copies, remote signals or barrier semaphores. Data moves between devices by JAX's collectives and lax.ppermute only.
A program may use at most 192 MiB of HBM per device.

v0:
```python
import jax
import jax.numpy as jnp
from jax import lax
from jax.sharding import PartitionSpec as P

LAGS = 5


sparsity_weight = 0.01


def shifted(block, axis, distance):
    devices = range(lax.axis_size(axis))
    route = [(i - distance, i) for i in devices if i - distance in devices]
    return lax.ppermute(block, axis, route)


def extended(block, sides, width):
    for axis, dim in sides:
        count = lax.axis_size(axis)
        forward = [(i, i + 1) for i in range(count - 1)]
        backward = [(target, source) for source, target in forward]
        low = lax.ppermute(
            lax.slice_in_dim(block, block.shape[dim] - width, None, axis=dim), axis, forward
        )
        high = lax.ppermute(lax.slice_in_dim(block, 0, width, axis=dim), axis, backward)
        block = jnp.concatenate([low, block, high], axis=dim)
    return block


def body(
    fields,
    cell_latent,
    enc_weight,
    dec_weight,
    trans_weight,
    graph_logits,
    hidden_bias,
    out_weight,
    noise_var,
):
    batch_size, step_count, var_count, cell_count = fields.shape
    lat_dev, hidden, lag_width = trans_weight.shape
    latent_count = lag_width // LAGS
    highest = lax.Precision.HIGHEST
    device = lax.axis_index(("space", "lat"))
    norm_factor = 1.0 / (batch_size * step_count)
    rows = batch_size * (step_count - LAGS)
    local_index = cell_latent - (device - 1) * lat_dev
    one_hot = (local_index[:, None] == jnp.arange(3 * lat_dev, dtype=jnp.int32)[None, :]).astype(
        jnp.float32
    )
    projected = jnp.sum(fields.astype(jnp.float32) * enc_weight[None, None], axis=2)
    enc_part = jnp.einsum("btc,cj->btj", projected, one_hot, precision=highest)
    spread_table = jnp.zeros((batch_size, step_count, latent_count + 2 * lat_dev), jnp.float32)
    spread_table = lax.dynamic_update_slice_in_dim(spread_table, enc_part, device * lat_dev, 2)
    latent_full = lax.psum(spread_table[:, :, lat_dev : latent_count + lat_dev], ("space", "lat"))
    own_latent = lax.dynamic_slice_in_dim(latent_full, device * lat_dev, lat_dev, 2)
    latent_bf = latent_full.astype(jnp.bfloat16)
    padded_latent = jnp.pad(latent_bf, ((0, 0), (0, 0), (lat_dev, lat_dev)))
    window = lax.dynamic_slice_in_dim(padded_latent, device * lat_dev, 3 * lat_dev, 2)
    cell_values = jnp.einsum("btj,cj->btc", window.astype(jnp.float32), one_hot, precision=highest)
    resid = dec_weight[None, None] * cell_values[:, :, None, :] - fields.astype(jnp.float32)
    grad_dec = norm_factor * jnp.einsum("btvc,btc->vc", resid, cell_values, precision=highest)
    cell_grad = norm_factor * jnp.sum(resid * dec_weight[None, None], axis=2)
    window_grad = jnp.einsum("btc,cj->btj", cell_grad, one_hot, precision=highest)
    lagged = jnp.stack(
        [latent_bf[:, LAGS - lag : step_count - lag, :] for lag in range(1, LAGS + 1)], axis=2
    )
    lagged = lagged.reshape(rows, lag_width)
    edge_prob = jax.nn.sigmoid(graph_logits)
    eff_weight = (trans_weight.astype(jnp.float32) * edge_prob[:, None, :]).astype(jnp.bfloat16)
    pre_act = (
        jnp.einsum("ri,kmi->rkm", lagged, eff_weight, preferred_element_type=jnp.float32)
        + hidden_bias[None]
    )
    gate_sig = jax.nn.sigmoid(pre_act)
    predicted = jnp.sum(pre_act * gate_sig * out_weight[None], axis=2)
    target = own_latent[:, LAGS:, :].reshape(rows, lat_dev)
    direct = norm_factor * (target - predicted) / noise_var[None]
    hidden_grad = (
        (-direct)[:, :, None] * out_weight[None] * gate_sig * (1.0 + pre_act * (1.0 - gate_sig))
    )
    hidden_bf = hidden_grad.astype(jnp.bfloat16)
    weight_grad = jnp.einsum("rkm,ri->kmi", hidden_bf, lagged, preferred_element_type=jnp.float32)
    grad_trans = (weight_grad * edge_prob[:, None, :]).astype(jnp.bfloat16)
    flip = edge_prob * (1.0 - edge_prob)
    grad_graph = (
        jnp.sum(weight_grad * trans_weight.astype(jnp.float32), axis=1) * flip
        + sparsity_weight * flip
    )
    input_grad = jnp.einsum(
        "rkm,kmi->ri", hidden_bf, eff_weight, preferred_element_type=jnp.float32
    )
    input_grad = input_grad.reshape(batch_size, step_count - LAGS, LAGS, latent_count)
    owned_terms = lax.psum_scatter(input_grad, ("space", "lat"), scatter_dimension=3, tiled=True)
    lag_grad = jnp.zeros((batch_size, step_count, lat_dev), jnp.float32)
    for lag in range(1, LAGS + 1):
        lag_grad = lag_grad + jnp.pad(
            owned_terms[:, :, lag - 1, :], ((0, 0), (LAGS - lag, lag), (0, 0))
        )
    grad_above = shifted(window_grad[:, :, :lat_dev], ("space", "lat"), -1)
    grad_below = shifted(window_grad[:, :, 2 * lat_dev :], ("space", "lat"), 1)
    direct_steps = jnp.pad(
        direct.reshape(batch_size, step_count - LAGS, lat_dev), ((0, 0), (LAGS, 0), (0, 0))
    )
    own_grad = (
        window_grad[:, :, lat_dev : 2 * lat_dev] + grad_above + grad_below + lag_grad + direct_steps
    )
    halo_grad = extended(own_grad, ((("space", "lat"), 2),), lat_dev)
    cell_total = jnp.einsum("btj,cj->btc", halo_grad, one_hot, precision=highest)
    grad_enc = jnp.einsum("btvc,btc->vc", fields.astype(jnp.float32), cell_total, precision=highest)
    return (grad_enc, grad_dec, grad_trans, grad_graph)


def solution(mesh):
    return jax.shard_map(
        body,
        mesh=mesh,
        in_specs=(
            P(None, None, None, ("space", "lat")),
            P(("space", "lat")),
            P(None, ("space", "lat")),
            P(None, ("space", "lat")),
            P(("space", "lat"), None, None),
            P(("space", "lat"), None),
            P(("space", "lat"), None),
            P(("space", "lat"), None),
            P(("space", "lat")),
        ),
        out_specs=(
            P(None, ("space", "lat")),
            P(None, ("space", "lat")),
            P(("space", "lat"), None, None),
            P(("space", "lat"), None),
        ),
        check_vma=False,
    )
```

profile of v0, /device:TPU:1, one launch (start us, length us, event | category | flops | bytes accessed | tf_op | source)
XLA Modules:
  0.0 460.4 jit_solution(15953483216375521314)
XLA Ops:
  7.2 0.7 broadcast_subtract_fusion
  7.9 2.8 fusion.9
  10.7 1.2 fusion.18
  11.9 0.1 broadcast_in_dim.2
  12.0 1.1 dynamic_update_slice.3
  13.1 1.3 slice.60
  14.5 0.2 add_divide_fusion.1
  14.7 131.0 %all-reduce.11.cloned.1.call-done = f32[4,64,1024]{2,1,0:T(8,128)} async-done(((f32[4,64,1024]{2,1,0:T(8,128)}), f32[4,64,1024]{2,1,0:T(8,128)}) %all-reduce.11.cloned.1.call-update) | async-done | bytes 1048592 | tf_op jit(solution)/shard_map/psum | solution.py:57
  145.7 1.4 convert_element_type.38
  147.2 0.5 fusion.16
  147.7 0.1 fusion.25
  147.8 0.1 copy-done
  147.9 1.1 multiply_reduce_fusion.2
  149.1 1.2 fusion.10
  150.3 0.8 fusion.43
  151.0 3.1 collective-permute-start.1
  154.1 3.3 collective-permute-start
  157.5 0.1 fusion.24
  157.6 0.1 fusion.23
  157.7 0.1 fusion.22
  157.9 3.4 copy.19
  161.3 6.8 %reshape.55 = bf16[236,5120,1]{1,0,2:T(8,128)(2,1)} reshape(bf16[4,59,5,1024]{3,2,1,0:T(8,128)(2,1)} %copy.19) | data formatting | bytes 4833280 | tf_op jit(solution)/shard_map/reshape | solution.py:70
  168.1 12.6 %multiply_reduce_fusion.3 = (f32[236,32]{0,1:T(8,128)}, f32[236,32,64]{0,2,1:T(8,128)}) fusion(f32[32,64]{1,0:T(8,128)} %param.16, f32[32,64]{1,0:T(8,128)} %param.15, bf16[236,5120,1]{1,0,2:T(8,128)(2,1)} %reshape.55, bf16[32,64,5120]{2,1,0:T(8,128)(2,1)} %param.13, f32[32,5120]{1,0:T(8,128)S(1)} %add_divide_fusion.1), kind=kOutput, calls=%fused_computation.16 | convolution fusion | flops 4984111616 | bytes 26023424 | tf_op jit(solution)/shard_map/ri,kmi->rkm/dot_general | solution.py:74
  180.7 1.5 reduce_sum.41
  182.1 1.6 copy.26
  183.8 1.8 multiply_divide_fusion
  185.5 1.6 copy.18
  187.2 1.5 reshape.51
  188.7 1.5 divide_negate_fusion
  190.2 16.1 %fusion.6 = f32[236,5120]{1,0:T(8,128)} fusion(bf16[32,64,5120]{2,1,0:T(8,128)(2,1)} %param.13, f32[32,5120]{1,0:T(8,128)S(1)} %add_divide_fusion.1, f32[236,32,64]{0,2,1:T(8,128)} %get-tuple-element.18, f32[236,32]{0,1:T(8,128)} %divide_negate_fusion, f32[32,64]{1,0:T(8,128)} %param.16, f32[32,64]{1,0:T(8,128)} %param.15), kind=kOutput, calls=%fused_computation.9 | convolution fusion | flops 4986052608 | bytes 28440064 | tf_op jit(solution)/shard_map/rkm,kmi->ri/dot_general | solution.py:92
  206.3 7.5 %reshape.53 = f32[4,59,5,1024]{3,2,1,0:T(8,128)} reshape(f32[236,5120]{1,0:T(8,128)} %fusion.6) | data formatting | bytes 9666560 | tf_op jit(solution)/shard_map/reshape | solution.py:95
  213.8 10.4 %copy.20 = f32[4,59,5,1024]{1,0,2,3:T(4,128)} copy(f32[4,59,5,1024]{3,2,1,0:T(8,128)} %reshape.53) | data formatting | bytes 9666560 | tf_op jit(solution)/shard_map/reshape | solution.py:95
  224.2 23.0 %fusion.1 = (f32[32,5120]{1,0:T(8,128)}, bf16[32,64,5120]{2,1,0:T(8,128)(2,1)}) fusion(bf16[32,64,5120]{2,1,0:T(8,128)(2,1)} %param.13, f32[32,5120]{1,0:T(8,128)S(1)} %add_divide_fusion.1, bf16[236,5120,1]{1,0,2:T(8,128)(2,1)} %reshape.55, f32[236,32,64]{0,2,1:T(8,128)} %get-tuple-element.18, f32[236,32]{0,1:T(8,128)} %divide_negate_fusion, ...), kind=kOutput, calls=%fused_computation.3 | convolution fusion | flops 5006860288 | bytes 47650304 | tf_op jit(solution)/shard_map/rkm,ri->kmi/dot_general | solution.py:85
  247.2 179.6 %all-reduce.13.cloned.1.call-done = f32[4,59,5,1024]{1,0,2,3:T(4,128)} async-done(((f32[4,59,5,1024]{1,0,2,3:T(4,128)}), f32[4,59,5,1024]{1,0,2,3:T(4,128)}) %all-reduce.13.cloned.1.call-update) | async-done | bytes 4833296
  426.8 1.7 constant_dynamic-slice_fusion.3
  428.6 1.6 copy.45
  430.1 1.6 copy.44
  431.8 1.6 copy.43
  433.4 1.6 copy.42
  435.0 1.6 copy.41
  436.6 1.4 fusion.32
  438.0 4.0 collective-permute-start.3
  442.0 1.9 collective-permute-start.2
  444.0 1.0 fusion.20
  445.0 4.7 %collective-permute-done.2 = f32[4,64,32]{2,1,0:T(8,128)S(1)} collective-permute-done((f32[4,64,32]{2,1,0:T(8,128)S(1)}, f32[4,64,32]{2,1,0:T(8,128)S(1)}, u32[]{:S(2)}, u32[]{:S(2)}) %collective-permute-start.2) | collective-permute-done | bytes 32800 | tf_op jit(solution)/shard_map/ppermute | solution.py:23
  449.7 1.0 convolution_bitcast_fusion
  450.7 2.2 multiply_reduce_fusion
  452.9 0.6 multiply_bitcast_fusion
  (21 shorter events, 0.2 us)
Async XLA Ops:
  7.2 138.6 %all-reduce.11.cloned.1.call-start = ((), (), s32[]{:S(2)}) async-start(), calls=%async_computation | async-start | bytes 2097152 | tf_op jit(solution)/shard_map/psum | solution.py:57
  11.9 2.6 copy-start.2
  14.5 412.4 %all-reduce.13.cloned.1.call-start = ((), (), s32[]{:S(2)}) async-start(), calls=%async_computation.1 | async-start | bytes 20971520
  14.7 133.1 %copy-start.4 = (f32[3,2048]{1,0:T(4,128)S(1)}, f32[3,2048]{1,0:T(4,128)}, u32[]{:S(2)}) copy-start(f32[3,2048]{1,0:T(4,128)} %param.12) | copy-start | bytes 73732
  145.7 2.2 copy-start
  151.0 285.5 %collective-permute-start.1 = (f32[4,64,32]{2,1,0:T(8,128)}, f32[4,64,32]{2,1,0:T(8,128)}, u32[]{:S(2)}, u32[]{:S(2)}) collective-permute-start(f32[4,64,32]{2,1,0:T(8,128)} %get-tuple-element.16), channel_id=1, source_target_pairs={{0,1},{1,2},{2,3},{3,4},{4,5},{5,6},{6,7},{7,8},{8,9},{9,10},{10,1... | collective-permute-start | bytes 98312 | tf_op jit(solution)/shard_map/ppermute | solution.py:15
  154.1 282.5 %collective-permute-start = (f32[4,64,32]{2,1,0:T(8,128)}, f32[4,64,32]{2,1,0:T(8,128)}, u32[]{:S(2)}, u32[]{:S(2)}) collective-permute-start(f32[4,64,32]{2,1,0:T(8,128)} %get-tuple-element.15), channel_id=1, source_target_pairs={{1,0},{2,1},{3,2},{4,3},{5,4},{6,5},{7,6},{8,7},{9,8},{10,9},{11,1... | collective-permute-start | bytes 98312 | tf_op jit(solution)/shard_map/ppermute | solution.py:15
  168.1 15.7 %copy-start.6 = (f32[32]{0:T(128)S(1)}, f32[32]{0:T(128)}, u32[]{:S(2)}) copy-start(f32[32]{0:T(128)} %param.17) | copy-start | bytes 388
  247.2 196.8 %copy-start.3 = (f32[32,5120]{1,0:T(8,128)S(1)}, f32[32,5120]{1,0:T(8,128)}, u32[]{:S(2)}) copy-start(f32[32,5120]{1,0:T(8,128)} %get-tuple-element.8) | copy-start | bytes 1966084
  438.0 12.7 %copy-start.1 = (bf16[4,64,3,2048]{3,1,2,0:T(8,128)(2,1)S(1)}, bf16[4,64,3,2048]{3,1,2,0:T(8,128)(2,1)}, u32[]{:S(2)}) copy-start(bf16[4,64,3,2048]{3,1,2,0:T(8,128)(2,1)} %param.9) | copy-start | bytes 9437188
  438.0 12.7 %copy-start.5 = (f32[3,2048]{1,0:T(4,128)S(1)}, f32[3,2048]{1,0:T(4,128)}, u32[]{:S(2)}) copy-start(f32[3,2048]{1,0:T(4,128)} %param.12) | copy-start | bytes 73732
  438.0 7.0 %collective-permute-start.3 = (f32[4,64,32]{2,1,0:T(8,128)S(1)}, f32[4,64,32]{2,1,0:T(8,128)S(1)}, u32[]{:S(2)}, u32[]{:S(2)}) collective-permute-start(f32[4,64,32]{2,1,0:T(8,128)S(1)} %fusion.32), channel_id=1, source_target_pairs={{1,0},{2,1},{3,2},{4,3},{5,4},{6,5},{7,6},{8,7},{9,8},{10,9},{11,1... | collective-permute-start | bytes 98312 | tf_op jit(solution)/shard_map/ppermute | solution.py:26
  442.0 7.6 %collective-permute-start.2 = (f32[4,64,32]{2,1,0:T(8,128)S(1)}, f32[4,64,32]{2,1,0:T(8,128)S(1)}, u32[]{:S(2)}, u32[]{:S(2)}) collective-permute-start(f32[4,64,32]{2,1,0:T(8,128)S(1)} %fusion.32), channel_id=1, source_target_pairs={{0,1},{1,2},{2,3},{3,4},{4,5},{5,6},{6,7},{7,8},{8,9},{9,10},{10,1... | collective-permute-start | bytes 98312 | tf_op jit(solution)/shard_map/ppermute | solution.py:23
Sparse Core Ops, SparseCore 0:
  14.6 131.1 all-reduce.10
  224.4 202.4 all-reduce.12
where the time goes:
time: 462 us; the launch traced here: 460 us
  waiting for transfers between devices  315 us (68%)
  matrix products  55.6 us (12%)
  local copies, waits for them, and re-layouts  48 us (10%)
  other arithmetic  14.7 us (3%)
  between operations  14.3 us (3%)
  starting transfers between devices  12.4 us (3%)
    unnamed x3, waiting for transfers between devices  180 us
    psum x1, waiting for transfers between devices, body(): lax.psum(spread_table[:, :, lat_dev:latent_count + lat_dev], ('space', 'l...  131 us
    dot_general x1, matrix products, body(): jnp.einsum('rkm,ri->kmi', hidden_bf, lagged, preferred_element_type=jnp.f...  23 us
    reshape x2, local copies, waits for them, and re-layouts, body(): input_grad.reshape(batch_size, step_count - LAGS, LAGS, latent_count)  17.9 us
    dot_general x1, matrix products, body(): jnp.einsum('rkm,kmi->ri', hidden_bf, eff_weight, preferred_element_type=j...  16.1 us
    dot_general x1, matrix products, body(): jnp.einsum('ri,kmi->rkm', lagged, eff_weight, preferred_element_type=jnp....  12.6 us
  transfers between devices with their start and end apart: 6, of which 3 were waited for; matrix products, arithmetic and copies ran while one was open for 22% of the time, Pallas kernels for 0%

commit v1 on v0

v1 whole, which is shorter than its diff:
```python
import functools

import jax
import jax.numpy as jnp
from jax import lax
from jax.experimental import pallas as pl
from jax.experimental.pallas import tpu as pltpu
from jax.sharding import PartitionSpec as P

LAGS = 5
AXES = ("space", "lat")
sparsity_weight = 0.01
f32 = jnp.float32
bf16 = jnp.bfloat16
MIB = 1 << 20


def params(mib):
    return pltpu.CompilerParams(vmem_limit_bytes=mib * MIB)


def nt_dot(a, b):
    return lax.dot_general(a, b, (((1,), (1,)), ((), ())), preferred_element_type=f32)


def pieces(x, count):
    out = []
    for _ in range(count):
        part = x.astype(bf16)
        out.append(part.astype(f32))
        x = x - out[-1]
    return out


def in_vmem(x):
    return pltpu.with_memory_space_constraint(x, pltpu.VMEM)


VMEM = pl.BlockSpec(memory_space=pltpu.VMEM)


def group_of(lat_dev):
    return 8 if lat_dev % 8 == 0 else lat_dev


def encode_kernel(loc_ref, enc_ref, dec_ref, fields_ref, enc_out, dec_out, sq_out):
    width, cells = enc_out.shape[0], loc_ref.shape[1]
    mask = lax.broadcasted_iota(jnp.int32, (width, cells), 0) == loc_ref[...]
    total, square = None, None
    for var in range(fields_ref.shape[0]):
        dec = dec_ref[var : var + 1, :]
        weights = [
            jnp.where(mask, part, 0.0).astype(bf16)
            for part in pieces(enc_ref[var : var + 1, :], 3) + pieces(dec, 2)
        ]
        part = nt_dot(jnp.concatenate(weights, axis=0), fields_ref[var])
        total = part if total is None else total + part
        square = dec * dec if square is None else square + dec * dec
    cut = [total[n * width : (n + 1) * width] for n in range(5)]
    enc_out[...] = cut[0] + (cut[1] + cut[2])
    dec_out[...] = cut[3] + cut[4]
    squares = jnp.sum(jnp.where(mask, square, 0.0), axis=1, keepdims=True)
    sq_out[...] = jnp.broadcast_to(squares, sq_out.shape)


def encode(loc, enc_weight, dec_weight, fields3, width):
    var_count, rows, cells = fields3.shape
    return pl.pallas_call(
        encode_kernel,
        in_specs=[VMEM] * 4,
        out_specs=[VMEM] * 3,
        out_shape=[jax.ShapeDtypeStruct((width, rows), f32)] * 3,
        compiler_params=params(12),
        cost_estimate=pl.CostEstimate(
            flops=50 * width * rows * cells * var_count,
            bytes_accessed=2 * rows * cells * var_count,
            transcendentals=0,
        ),
        name="encode",
    )(loc, enc_weight, dec_weight, fields3)


def edge_kernel(group, first, logit_ref, weight_ref, out_ref):
    hidden = weight_ref.shape[1]
    for k in range(group):
        edge = jax.nn.sigmoid(logit_ref[first + k : first + k + 1, :])
        out_ref[k * hidden : (k + 1) * hidden, :] = (
            weight_ref[first + k].astype(f32) * edge
        ).astype(bf16)


def effective(logits, weights, part):
    lat_dev, hidden, lag_width = weights.shape
    group = group_of(lat_dev)
    out = pl.pallas_call(
        functools.partial(edge_kernel, group, part * group),
        in_specs=[VMEM] * 2,
        out_specs=VMEM,
        out_shape=jax.ShapeDtypeStruct((group * hidden, lag_width), bf16),
        compiler_params=params(2),
        cost_estimate=pl.CostEstimate(
            flops=2 * group * hidden * lag_width,
            bytes_accessed=4 * group * hidden * lag_width,
            transcendentals=0,
        ),
        name="effective",
    )(logits, weights)
    return in_vmem(out)


def transition_kernel(steps, norm, order, inverse, parts, device_ref, lat_ref, own_ref, bias_ref,
                      out_w_ref, var_ref, dec_ref, sq_ref, *refs):
    eff = refs[:parts]
    hid_out, lagged_out, grad_out, direct_out, window_out, lagged, pre, hid_t, folded = refs[parts:]
    blocks, size, rows = lat_ref.shape
    latents = blocks * size
    span, lag_width = eff[0].shape
    lat_dev, hidden = bias_ref.shape
    group = span // hidden
    device = device_ref[0]

    def spot(block):
        found = jnp.int32(0)
        for bit, moved in inverse:
            found = found | (((block >> bit) & 1) << moved)
        return found

    for p in range(blocks):
        values = lat_ref[p].astype(f32)
        at = pl.multiple_of((device ^ order[p]) * size, size) if blocks > 1 else 0
        for lag in range(1, LAGS + 1):
            turned = pltpu.roll(values, lag, 1).astype(bf16)
            lagged[pl.ds((lag - 1) * latents + at, size), :] = turned

    bias_t, out_w_t, var_t = bias_ref[...].T, out_w_ref[...].T, var_ref[...].T
    column = lax.broadcasted_iota(jnp.int32, (group, rows), 1)
    valid = lax.rem(column, steps) >= LAGS
    for part in range(parts):
        pre[...] = jnp.dot(eff[part][...], lagged[...], preferred_element_type=f32)
        first = part * group
        for k in range(group):
            value = pre[k * hidden : (k + 1) * hidden, :] + bias_t[:, first + k : first + k + 1]
            out_w = out_w_t[:, first + k : first + k + 1]
            gate = jax.nn.sigmoid(value)
            direct_out[first + k : first + k + 1, :] = jnp.sum(
                value * gate * out_w, axis=0, keepdims=True
            )
            pre[k * hidden : (k + 1) * hidden, :] = out_w * gate * (1.0 + value * (1.0 - gate))
        at = slice(first, first + group)
        direct = norm * (own_ref[at, :] - direct_out[at, :]) / var_t[at, :]
        direct = jnp.where(valid, direct, 0.0)
        direct_out[at, :] = direct
        for k in range(group):
            here = slice(k * hidden, (k + 1) * hidden)
            slope = pre[here, :] * (-direct[k : k + 1, :])
            hid_out[part * span + k * hidden : part * span + (k + 1) * hidden, :] = slope.astype(bf16)
            pre[here, :] = slope
        hid_t[:, part * span : (part + 1) * span] = pre[...].T.astype(bf16)

    for lag in range(1, LAGS + 1):
        at = slice((lag - 1) * latents, lag * latents)
        lagged_out[:, at] = lagged[at, :].astype(f32).T.astype(bf16)
        term = None
        for part in range(parts):
            more = jnp.dot(
                hid_t[:, part * span : (part + 1) * span],
                eff[part][:, at],
                preferred_element_type=f32,
            )
            term = more if term is None else term + more
        term = pltpu.roll(term, rows - lag, 0)
        folded[...] = term if lag == 1 else folded[...] + term
    total = folded[...].T
    if blocks == 1:
        grad_out[0] = total
        return
    here = spot(device)
    for block in range(blocks):
        at = sum(((block >> bit) & 1) << moved for bit, moved in inverse)
        grad_out[at ^ here] = total[block * size : (block + 1) * size]
    grad_out[0] += direct_out[...]
    below = spot(jnp.maximum(device - 1, 0)) ^ here
    above = spot(jnp.minimum(device + 1, blocks - 1)) ^ here
    for n, at in ((0, below), (1, 0), (2, above)):
        part = slice(n * size, (n + 1) * size)
        values = lat_ref[at]
        window_out[part, :] = values
        grad_out[at] += norm * (values.astype(f32) * sq_ref[part, :] - dec_ref[part, :])


def transition(steps, norm, order, inverse, device, lat3, own, bias, out_w, var, dec_sums, squares, eff):
    blocks, size, rows = lat3.shape
    lat_dev, hidden = bias.shape
    span, lag_width = eff[0].shape
    km = lat_dev * hidden
    shape = jax.ShapeDtypeStruct
    return pl.pallas_call(
        functools.partial(transition_kernel, steps, norm, order, inverse, len(eff)),
        in_specs=[pl.BlockSpec(memory_space=pltpu.SMEM)] + [VMEM] * (7 + len(eff)),
        out_specs=[VMEM] * 5,
        out_shape=[
            shape((km, rows), bf16),
            shape((rows, lag_width), bf16),
            shape((blocks, size, rows), f32),
            shape((lat_dev, rows), f32),
            shape(dec_sums.shape, bf16),
        ],
        scratch_shapes=[
            pltpu.VMEM((lag_width, rows), bf16),
            pltpu.VMEM((span, rows), f32),
            pltpu.VMEM((rows, km), bf16),
            pltpu.VMEM((rows, blocks * size), f32),
        ],
        compiler_params=params(9),
        cost_estimate=pl.CostEstimate(
            flops=4 * km * lag_width * rows,
            bytes_accessed=2 * km * lag_width,
            transcendentals=km * rows,
        ),
        name="transition",
    )(device, lat3, own, bias, out_w, var, dec_sums, squares, *eff)


def weight_kernel(start, hid_ref, lagged_ref, logit_ref, weight_ref, *refs):
    trans_out, graph_out, work = refs[-3:]
    lat_dev, hidden, lag_width = weight_ref.shape
    tile = lagged_ref.shape[1]
    group = group_of(lat_dev)
    at = pl.multiple_of(start + pl.program_id(0) * tile, tile)
    for g in range(lat_dev // group):
        held = work.at[g % 2]
        held[...] = jnp.dot(
            hid_ref[g * group * hidden : (g + 1) * group * hidden, :],
            lagged_ref[...],
            preferred_element_type=f32,
        )
        for k in range(group):
            n = g * group + k
            edge = jax.nn.sigmoid(logit_ref[n : n + 1, :])
            grad = held[k * hidden : (k + 1) * hidden, :]
            trans_out[n] = (grad * edge).astype(bf16)
            flip = edge * (1.0 - edge)
            value = weight_ref[n, :, pl.ds(at, tile)].astype(f32)
            total = jnp.sum(grad * value, axis=0, keepdims=True)
            graph_out[n : n + 1, :] = total * flip + sparsity_weight * flip


def weight_grads(hid, lagged, logits, weights, first, count, held):
    lat_dev, hidden, lag_width = weights.shape
    km, rows = hid.shape
    tile = TILE
    group = group_of(lat_dev)
    skip = first // tile
    two = pl.BlockSpec((lat_dev, tile), lambda i: (0, i + skip))
    held = list(held)
    return pl.pallas_call(
        functools.partial(weight_kernel, first),
        grid=(count // tile,),
        in_specs=[
            pl.BlockSpec((km, rows), lambda i: (0, 0)),
            pl.BlockSpec((rows, tile), lambda i: (0, i + skip)),
            two,
            VMEM,
        ]
        + [pl.BlockSpec(memory_space=pl.ANY)] * len(held),
        out_specs=[pl.BlockSpec((lat_dev, hidden, tile), lambda i: (0, 0, i + skip)), two],
        out_shape=[
            jax.ShapeDtypeStruct(weights.shape, bf16),
            jax.ShapeDtypeStruct((lat_dev, lag_width), f32),
        ],
        scratch_shapes=[pltpu.VMEM((2, group * hidden, tile), f32)],
        input_output_aliases={4 + n: n for n in range(len(held))},
        compiler_params=params(16),
        cost_estimate=pl.CostEstimate(
            flops=2 * km * count * rows, bytes_accessed=4 * km * count, transcendentals=0
        ),
        name="weight_grads",
    )(hid, lagged, logits, weights, *held)


TILE = 256


def pick(mask, table, fields):
    both = jnp.dot(table, fields, preferred_element_type=f32)
    return jnp.sum(jnp.where(mask, both, 0.0), axis=0, keepdims=True)


def mask_of(loc_ref, width):
    return lax.broadcasted_iota(jnp.int32, (width, loc_ref.shape[1]), 0) == loc_ref[...]


def grad_dec_kernel(norm, loc_ref, win_ref, dec_ref, fields_ref, out_ref):
    values = win_ref[...]
    mask = mask_of(loc_ref, values.shape[0])
    wide = values.astype(f32)
    power = jnp.sum(wide * wide, axis=1, keepdims=True)
    power = jnp.sum(jnp.where(mask, power, 0.0), axis=0, keepdims=True)
    for var in range(fields_ref.shape[0]):
        cross = pick(mask, values, fields_ref[var])
        out_ref[var : var + 1, :] = norm * (dec_ref[var : var + 1, :] * power - cross)


def grad_enc_kernel(loc_ref, grad_ref, fields_ref, out_ref):
    high, low = (part.astype(bf16) for part in pieces(grad_ref[...], 2))
    mask = mask_of(loc_ref, high.shape[0])
    for var in range(fields_ref.shape[0]):
        out_ref[var : var + 1, :] = pick(mask, high, fields_ref[var]) + pick(
            mask, low, fields_ref[var]
        )


def cell_call(kernel, loc, table, extras, fields3, name):
    var_count, rows, cells = fields3.shape
    return pl.pallas_call(
        kernel,
        in_specs=[VMEM] * (3 + len(extras)),
        out_specs=VMEM,
        out_shape=jax.ShapeDtypeStruct((var_count, cells), f32),
        compiler_params=params(12),
        cost_estimate=pl.CostEstimate(
            flops=4 * table.shape[0] * rows * cells * var_count,
            bytes_accessed=2 * rows * cells * var_count,
            transcendentals=0,
        ),
        name=name,
    )(loc, table, *extras, fields3)


def paired(block, device, count, first):
    route = []
    for low in range(first, count - 1, 2):
        route += [(low, low + 1), (low + 1, low)]
    return lax.ppermute(block, AXES, route)


def from_neighbours(down, up, device, count):
    even = lax.rem(device, 2) == 0
    first = paired(jnp.where(even, up, down), device, count, 0)
    second = paired(jnp.where(even, down, up), device, count, 1)
    return first, second, even


def body(
    fields,
    cell_latent,
    enc_weight,
    dec_weight,
    trans_weight,
    graph_logits,
    hidden_bias,
    out_weight,
    noise_var,
):
    batch_size, step_count, var_count, cell_count = fields.shape
    lat_dev, hidden, lag_width = trans_weight.shape
    latent_count = lag_width // LAGS
    rows = batch_size * step_count
    norm = 1.0 / rows
    width = 3 * lat_dev
    space, lat = lax.axis_size("space"), lax.axis_size("lat")
    count = space * lat
    device = lax.axis_index(AXES)
    doubling = count & (count - 1) == 0 and lat_dev % 16 == 0
    bits = [n for n in range(count.bit_length() - 2, -1, -1)]
    core = lat.bit_length() - 1
    bits = [n for n in bits if n != core] + [core]

    loc = (cell_latent - (device - 1) * lat_dev)[None]
    fields3 = jnp.transpose(fields.reshape(rows, var_count, cell_count), (1, 0, 2))
    enc_sums, dec_sums, squares = encode(loc, enc_weight, dec_weight, fields3, width)
    first, second, even = from_neighbours(
        enc_sums[:lat_dev], enc_sums[2 * lat_dev :], device, count
    )
    held_weights = in_vmem(trans_weight)
    parts = lat_dev // group_of(lat_dev)
    eff = []

    def beside(value, after):
        if len(eff) == parts:
            return value
        logits, _ = lax.optimization_barrier((graph_logits, after))
        value, made = lax.optimization_barrier(
            (value, effective(logits, held_weights, len(eff)))
        )
        eff.append(made)
        return value


    own = enc_sums[lat_dev : 2 * lat_dev] + first + second
    own_bf = own.astype(bf16)

    if doubling:
        gathered = own_bf[None]
        for bit in bits:
            route = [(n, n ^ (1 << bit)) for n in range(count)]
            got = beside(lax.ppermute(gathered, AXES, route), gathered)
            gathered = jnp.concatenate([gathered, got], axis=0)
        order = [0]
        for bit in bits:
            order = order + [n ^ (1 << bit) for n in order]
        inverse = [(bit, n) for n, bit in enumerate(bits)]
    else:
        order, inverse = [0], []
        gathered = lax.all_gather(own_bf, AXES, axis=0, tiled=True)
        padded = jnp.pad(gathered, ((lat_dev, lat_dev), (0, 0)))
        window = lax.dynamic_slice_in_dim(padded, device * lat_dev, width, 0)
        gathered = gathered[None]

    while len(eff) < parts:
        gathered = beside(gathered, enc_sums)
    eff = [in_vmem(part) for part in eff]
    hid, lagged, partial, direct, seen = transition(
        step_count, norm, order, inverse, device.astype(jnp.int32)[None], gathered, own,
        hidden_bias, out_weight, noise_var[None], dec_sums, squares, eff,
    )
    window = seen if doubling else window

    if doubling:
        held = []
        total = partial
        fillers = LAGS if lag_width // LAGS % 256 == 0 else 1
        chunk = lag_width // fillers
        done = 0
        for n, bit in enumerate(reversed(bits)):
            half = total.shape[0] // 2
            route = [(m, m ^ (1 << bit)) for m in range(count)]
            got = lax.ppermute(total[half:].astype(bf16), AXES, route)
            if done < fillers:
                held = weight_grads(
                    hid, lagged, graph_logits, held_weights, done * chunk, chunk, held
                )
                done += 1
            total = total[:half] + got.astype(f32)
        while done < fillers:
            held = weight_grads(hid, lagged, graph_logits, held_weights, done * chunk, chunk, held)
            done += 1
        own_grad = total[0]
        grad_trans, grad_graph = held
    else:
        grad_trans, grad_graph = weight_grads(
            hid, lagged, graph_logits, held_weights, 0, lag_width, []
        )
        extra = norm * (window.astype(f32) * squares - dec_sums)
        extra = extra + jnp.pad(direct, ((lat_dev, lat_dev), (0, 0)))
        table = jnp.zeros((latent_count + 2 * lat_dev, rows), f32)
        table = lax.dynamic_update_slice_in_dim(table, extra, device * lat_dev, 0)
        partial = partial[0] + table[lat_dev : lat_dev + latent_count]
        own_grad = lax.psum_scatter(partial, AXES, scatter_dimension=0, tiled=True)

    grad_dec = cell_call(
        functools.partial(grad_dec_kernel, norm), loc, window, [dec_weight], fields3, "grad_dec"
    )
    first, second, even = from_neighbours(own_grad, own_grad, device, count)
    grad_window = jnp.concatenate(
        [jnp.where(even, second, first), own_grad, jnp.where(even, first, second)], axis=0
    )
    grad_enc = cell_call(grad_enc_kernel, loc, grad_window, [], fields3, "grad_enc")
    return (grad_enc, grad_dec, grad_trans, grad_graph)


def solution(mesh):
    return jax.shard_map(
        body,
        mesh=mesh,
        in_specs=(
            P(None, None, None, AXES),
            P(AXES),
            P(None, AXES),
            P(None, AXES),
            P(AXES, None, None),
            P(AXES, None),
            P(AXES, None),
            P(AXES, None),
            P(AXES),
        ),
        out_specs=(
            P(None, AXES),
            P(None, AXES),
            P(AXES, None, None),
            P(AXES, None),
        ),
        check_vma=False,
    )
```

time: 462 us -> 83.3 us (0.18)
  waiting for transfers between devices: 315 us -> 9.28 us
  matrix products: 55.6 us -> 0 us
  local copies, waits for them, and re-layouts: 48 us -> 2.46 us
  Pallas kernels: 0 us -> 41.6 us
  starting transfers between devices: 12.4 us -> 27.7 us
  other arithmetic: 14.7 us -> 0.19 us
  between operations: 14.3 us -> 0.94 us
    unnamed x3 -> x0, waiting for transfers between devices: 180 us -> none
    psum x1 -> x0, waiting for transfers between devices: 131 us -> none  [body(): lax.psum(spread_table[:, :, lat_dev:latent_count + lat_dev], ('space', 'l...]
    dot_general x7 -> x0, matrix products: 55.6 us -> none  [the longest x1 23 us: body(): jnp.einsum('rkm,ri->kmi', hidden_bf, lagged, preferred_element_type=jnp.f...]
    pallas_call x0 -> x13, Pallas kernels: none -> 41.6 us  [the longest x5 19.4 us: weight_grads(): pl.pallas_call(functools.partial(weight_kernel, first), grid=(count // ti...]
    reshape x4 -> x0, local copies, waits for them, and re-layouts: 26.2 us -> none  [the longest x2 17.9 us: body(): input_grad.reshape(batch_size, step_count - LAGS, LAGS, latent_count)]
    ppermute x4 -> x14, starting transfers between devices: 12.3 us -> 27.7 us  [the longest x5 12.7 us: body(): got = beside(lax.ppermute(gathered, AXES, route), gathered)]
    unnamed x23 -> x21, local copies, waits for them, and re-layouts: 8.67 us -> 2.36 us
    slice x4 -> x5, local copies, waits for them, and re-layouts: 5.4 us -> 0.07 us  [body(): got = lax.ppermute(total[half:].astype(bf16), AXES, route)]
  transfers between devices with their start and end apart: 6 -> 14, of which waited for: 3 -> 8; matrix products, arithmetic and copies ran while one was open for 22% -> 0% of each run, Pallas kernels for 0% -> 30%
where the time goes in v1:
time: 83.3 us; the launch traced here: 82.1 us
  Pallas kernels  41.6 us (50%)
  starting transfers between devices  27.7 us (33%)
  waiting for transfers between devices  9.28 us (11%)
  local copies, waits for them, and re-layouts  2.46 us (3%)
  between operations  0.94 us (1%)
    pallas_call x5, Pallas kernels, weight_grads(): pl.pallas_call(functools.partial(weight_kernel, first), grid=(count // ti...  19.4 us
    pallas_call x1, Pallas kernels, transition(): pl.pallas_call(functools.partial(transition_kernel, steps, norm, order, i...  13.5 us
    ppermute x5, starting transfers between devices, body(): got = beside(lax.ppermute(gathered, AXES, route), gathered)  12.7 us
    ppermute x4, starting transfers between devices, paired(): return lax.ppermute(block, AXES, route)  10 us
    ppermute x5, waiting for transfers between devices, body(): got = beside(lax.ppermute(gathered, AXES, route), gathered)  5.1 us
    ppermute x5, starting transfers between devices, body(): got = lax.ppermute(total[half:].astype(bf16), AXES, route)  4.94 us
    pallas_call x4, Pallas kernels, effective(): pl.pallas_call(functools.partial(edge_kernel, group, part * group), in_sp...  3.71 us
    pallas_call x2, Pallas kernels, cell_call(): pl.pallas_call(kernel, in_specs=[VMEM] * (3 + len(extras)), out_specs=VME...  3.25 us
  transfers between devices with their start and end apart: 14, of which 8 were waited for; matrix products, arithmetic and copies ran while one was open for 0% of the time, Pallas kernels for 30%

profile of v1, /device:TPU:1, one launch (start us, length us, event | category | flops | bytes accessed | tf_op | source)
XLA Modules:
  0.0 82.1 jit_solution(15687357967366633979)
XLA Ops:
  0.6 0.0 copy-start.7
  0.6 0.0 copy-start.2
  0.7 2.3 %copy.21 = bf16[4,64,3,2048]{3,1,0,2:T(8,128)(2,1)S(1)} copy(bf16[4,64,3,2048]{3,1,2,0:T(8,128)(2,1)} %param.9) | data formatting | bytes 6291456 | tf_op args[0]
  3.0 0.0 copy-start
  3.0 0.0 copy-start.1
  3.0 1.7 %encode.1 = (f32[96,256]{1,0:T(8,128)S(1)}, f32[96,256]{1,0:T(8,128)S(1)}, f32[96,256]{1,0:T(8,128)S(1)}) custom-call(s32[1,2048]{1,0:T(1,128)S(1)} %bitcast.14, f32[3,2048]{1,0:T(4,128)S(1)} %copy-done.3, f32[3,2048]{1,0:T(4,128)S(1)} %copy-done.2, bf16[3,256,2048]{2,1,0:T(8,128)(2,1)S(1)} %bitcast.11), custom_call_target="tpu_custom_call" | custom-call | flops 7549747200 | bytes 3145728 | tf_op jit(solution)/shard_map/encode/pallas_call | solution.py:68
  4.8 2.1 %collective-permute-start = (f32[32,256]{1,0:T(8,128)S(1)}, f32[32,256]{1,0:T(8,128)S(1)}, u32[]{:S(2)}, u32[]{:S(2)}) collective-permute-start(f32[32,256]{1,0:T(8,128)S(1)} %get-tuple-element.67), channel_id=1, source_target_pairs={{0,1},{1,0},{2,3},{3,2},{4,5},{5,4},{6,7},{7,6},{8,9},{9,8},{10,11... | collective-permute-start | bytes 98312 | tf_op jit(solution)/shard_map/ppermute | solution.py:334
  6.9 2.9 %collective-permute-start.1 = (f32[32,256]{1,0:T(8,128)S(1)}, f32[32,256]{1,0:T(8,128)S(1)}, u32[]{:S(2)}, u32[]{:S(2)}) collective-permute-start(f32[32,256]{1,0:T(8,128)S(1)} %get-tuple-element.68), channel_id=1, source_target_pairs={{1,2},{2,1},{3,4},{4,3},{5,6},{6,5},{7,8},{8,7},{9,10},{10,9},{11,... | collective-permute-start | bytes 98312 | tf_op jit(solution)/shard_map/ppermute | solution.py:334
  9.8 0.0 collective-permute-done
  9.8 2.7 %collective-permute-done.1 = f32[32,256]{1,0:T(8,128)S(1)} collective-permute-done((f32[32,256]{1,0:T(8,128)S(1)}, f32[32,256]{1,0:T(8,128)S(1)}, u32[]{:S(2)}, u32[]{:S(2)}) %collective-permute-start.1) | collective-permute-done | bytes 32800 | tf_op jit(solution)/shard_map/ppermute | solution.py:334
  12.6 2.4 %collective-permute-start.2 = (bf16[1,32,256]{2,1,0:T(8,128)(2,1)S(1)}, bf16[1,32,256]{2,1,0:T(8,128)(2,1)S(1)}, u32[]{:S(2)}, u32[]{:S(2)}) collective-permute-start(bf16[1,32,256]{2,1,0:T(8,128)(2,1)S(1)} %get-tuple-element.63), channel_id=1, source_target_pairs={{0,16},{1,17},{2,18},{3,19},{4,20},{5,21},{6,22},{7,23},{8,24},{9,... | collective-permute-start | bytes 49160 | tf_op jit(solution)/shard_map/ppermute | solution.py:397
  14.9 0.9 %effective.4.refs_0_ = bf16[512,5120]{1,0:T(8,128)(2,1)S(1)} custom-call(f32[32,5120]{1,0:T(8,128)S(1)} %copy-done.1, bf16[32,64,5120]{2,1,0:T(8,128)(2,1)S(1)} %copy-done), custom_call_target="tpu_custom_call" | custom-call | flops 5242880 | bytes 10485760 | tf_op jit(solution)/shard_map/effective/pallas_call | solution.py:95
  15.9 0.2 collective-permute-done.2
  16.1 1.3 %collective-permute-start.3 = (bf16[2,32,256]{2,1,0:T(8,128)(2,1)S(1)}, bf16[2,32,256]{2,1,0:T(8,128)(2,1)S(1)}, u32[]{:S(2)}, u32[]{:S(2)}) collective-permute-start(bf16[2,32,256]{2,1,0:T(8,128)(2,1)S(1)} %pad_maximum_fusion.3), channel_id=1, source_target_pairs={{0,8},{1,9},{2,10},{3,11},{4,12},{5,13},{6,14},{7,15},{8,0},{9,1},... | collective-permute-start | bytes 98312 | tf_op jit(solution)/shard_map/ppermute | solution.py:397
  17.4 0.9 %effective.5.refs_1_ = bf16[512,5120]{1,0:T(8,128)(2,1)S(1)} custom-call(f32[32,5120]{1,0:T(8,128)S(1)} %copy-done.1, bf16[32,64,5120]{2,1,0:T(8,128)(2,1)S(1)} %copy-done), custom_call_target="tpu_custom_call" | custom-call | flops 5242880 | bytes 10485760 | tf_op jit(solution)/shard_map/effective/pallas_call | solution.py:95
  18.3 0.8 collective-permute-done.3
  19.2 1.0 %collective-permute-start.4 = (bf16[4,32,256]{2,1,0:T(8,128)(2,1)S(1)}, bf16[4,32,256]{2,1,0:T(8,128)(2,1)S(1)}, u32[]{:S(2)}, u32[]{:S(2)}) collective-permute-start(bf16[4,32,256]{2,1,0:T(8,128)(2,1)S(1)} %pad_maximum_fusion.2), channel_id=1, source_target_pairs={{0,4},{1,5},{2,6},{3,7},{4,0},{5,1},{6,2},{7,3},{8,12},{9,13},{10,... | collective-permute-start | bytes 196616 | tf_op jit(solution)/shard_map/ppermute | solution.py:397
  20.2 0.9 %effective.6.refs_2_ = bf16[512,5120]{1,0:T(8,128)(2,1)S(1)} custom-call(f32[32,5120]{1,0:T(8,128)S(1)} %copy-done.1, bf16[32,64,5120]{2,1,0:T(8,128)(2,1)S(1)} %copy-done), custom_call_target="tpu_custom_call" | custom-call | flops 5242880 | bytes 10485760 | tf_op jit(solution)/shard_map/effective/pallas_call | solution.py:95
  21.1 1.2 %collective-permute-done.4 = bf16[4,32,256]{2,1,0:T(8,128)(2,1)S(1)} collective-permute-done((bf16[4,32,256]{2,1,0:T(8,128)(2,1)S(1)}, bf16[4,32,256]{2,1,0:T(8,128)(2,1)S(1)}, u32[]{:S(2)}, u32[]{:S(2)}) %collective-permute-start.4) | collective-permute-done | bytes 65568 | tf_op jit(solution)/shard_map/ppermute | solution.py:397
  22.4 1.9 %collective-permute-start.5 = (bf16[8,32,256]{2,1,0:T(8,128)(2,1)S(1)}, bf16[8,32,256]{2,1,0:T(8,128)(2,1)S(1)}, u32[]{:S(2)}, u32[]{:S(2)}) collective-permute-start(bf16[8,32,256]{2,1,0:T(8,128)(2,1)S(1)} %pad_maximum_fusion), channel_id=1, source_target_pairs={{0,1},{1,0},{2,3},{3,2},{4,5},{5,4},{6,7},{7,6},{8,9},{9,8},{10,11... | collective-permute-start | bytes 393224 | tf_op jit(solution)/shard_map/ppermute | solution.py:397
  24.3 0.0 copy-start.6
  24.3 0.9 %effective.7.refs_3_ = bf16[512,5120]{1,0:T(8,128)(2,1)S(1)} custom-call(f32[32,5120]{1,0:T(8,128)S(1)} %copy-done.1, bf16[32,64,5120]{2,1,0:T(8,128)(2,1)S(1)} %copy-done), custom_call_target="tpu_custom_call" | custom-call | flops 5242880 | bytes 10485760 | tf_op jit(solution)/shard_map/effective/pallas_call | solution.py:95
  25.3 1.7 %collective-permute-done.5 = bf16[8,32,256]{2,1,0:T(8,128)(2,1)S(1)} collective-permute-done((bf16[8,32,256]{2,1,0:T(8,128)(2,1)S(1)}, bf16[8,32,256]{2,1,0:T(8,128)(2,1)S(1)}, u32[]{:S(2)}, u32[]{:S(2)}) %collective-permute-start.5) | collective-permute-done | bytes 131104 | tf_op jit(solution)/shard_map/ppermute | solution.py:397
  27.0 6.1 %collective-permute-start.6 = (bf16[16,32,256]{2,1,0:T(8,128)(2,1)S(1)}, bf16[16,32,256]{2,1,0:T(8,128)(2,1)S(1)}, u32[]{:S(2)}, u32[]{:S(2)}) collective-permute-start(bf16[16,32,256]{2,1,0:T(8,128)(2,1)S(1)} %get-tuple-element.65), channel_id=1, source_target_pairs={{0,2},{1,3},{2,0},{3,1},{4,6},{5,7},{6,4},{7,5},{8,10},{9,11},{10,... | collective-permute-start | bytes 786440 | tf_op jit(solution)/shard_map/ppermute | solution.py:397
  33.1 1.2 %collective-permute-done.6 = bf16[16,32,256]{2,1,0:T(8,128)(2,1)S(1)} collective-permute-done((bf16[16,32,256]{2,1,0:T(8,128)(2,1)S(1)}, bf16[16,32,256]{2,1,0:T(8,128)(2,1)S(1)}, u32[]{:S(2)}, u32[]{:S(2)}) %collective-permute-start.6) | collective-permute-done | bytes 262176 | tf_op jit(solution)/shard_map/ppermute | solution.py:397
  34.3 13.5 %transition.1 = (bf16[2048,256]{1,0:T(8,128)(2,1)S(1)}, bf16[256,5120]{1,0:T(8,128)(2,1)S(1)}, f32[32,32,256]{2,1,0:T(8,128)S(1)}, f32[32,256]{1,0:T(8,128)}, bf16[96,256]{1,0:T(8,128)(2,1)S(1)}) custom-call(s32[1]{0:T(128)} %bitcast.1.device_ref, bf16[32,32,256]{2,1,0:T(8,128)(2,1)S(1)} %constant_dynamic-update-slice_fusion.5.lat_ref, ...), custom_call_target="tpu_custom_call" | custom-call | flops 10737418240 | bytes 20971520 | tf_op jit(solution)/shard_map/transition/pallas_call | solution.py:197
  47.8 0.4 collective-permute-start.7
  48.2 1.2 %collective-permute-done.7 = bf16[16,32,256]{2,1,0:T(8,128)(2,1)S(1)} collective-permute-done((bf16[16,32,256]{2,1,0:T(8,128)(2,1)S(1)}, bf16[16,32,256]{2,1,0:T(8,128)(2,1)S(1)}, u32[]{:S(2)}, u32[]{:S(2)}) %collective-permute-start.7) | collective-permute-done | bytes 262176 | tf_op jit(solution)/shard_map/ppermute | solution.py:428
  49.4 0.1 convert_add_fusion
  49.5 0.1 collective-permute-start.8
  49.6 3.9 %weight_grads.5 = (bf16[32,64,5120]{2,1,0:T(8,128)(2,1)}, f32[32,5120]{1,0:T(8,128)}) custom-call(bf16[2048,256]{1,0:T(8,128)(2,1)S(1)} %get-tuple-element.50.hid_ref, bf16[256,5120]{1,0:T(8,128)(2,1)S(1)} %get-tuple-element.51.lagged_ref, f32[32,5120]{1,0:T(8,128)S(1)} %copy-done.1, bf16[32,64,5120]{2,1,0:T(8,128)(2,1)S(1)} %copy-done), custom_call_target="tpu_custom_call" | custom-call | flops 1073741824 | bytes 8388608 | tf_op jit(solution)/shard_map/weight_grads/pallas_call | solution.py:256
  53.4 3.9 %weight_grads.6 = (bf16[32,64,5120]{2,1,0:T(8,128)(2,1)}, f32[32,5120]{1,0:T(8,128)}) custom-call(bf16[2048,256]{1,0:T(8,128)(2,1)S(1)} %get-tuple-element.50.hid_ref, bf16[256,5120]{1,0:T(8,128)(2,1)S(1)} %get-tuple-element.51.lagged_ref, f32[32,5120]{1,0:T(8,128)S(1)} %copy-done.1, ...), custom_call_target="tpu_custom_call", output_to_operand_aliasing={{0}: (4, {}), {1}: (5, {})} | custom-call | flops 1073741824 | bytes 8388608 | tf_op jit(solution)/shard_map/weight_grads/pallas_call | solution.py:256
  57.3 0.0 collective-permute-done.8
  57.4 0.6 collective-permute-start.9
  58.0 3.9 %weight_grads.7 = (bf16[32,64,5120]{2,1,0:T(8,128)(2,1)}, f32[32,5120]{1,0:T(8,128)}) custom-call(bf16[2048,256]{1,0:T(8,128)(2,1)S(1)} %get-tuple-element.50.hid_ref, bf16[256,5120]{1,0:T(8,128)(2,1)S(1)} %get-tuple-element.51.lagged_ref, f32[32,5120]{1,0:T(8,128)S(1)} %copy-done.1, ...), custom_call_target="tpu_custom_call", output_to_operand_aliasing={{0}: (4, {}), {1}: (5, {})} | custom-call | flops 1073741824 | bytes 8388608 | tf_op jit(solution)/shard_map/weight_grads/pallas_call | solution.py:256
  61.9 0.0 collective-permute-done.9
  61.9 1.4 %collective-permute-start.10 = (bf16[2,32,256]{2,1,0:T(8,128)(2,1)S(1)}, bf16[2,32,256]{2,1,0:T(8,128)(2,1)S(1)}, u32[]{:S(2)}, u32[]{:S(2)}) collective-permute-start(bf16[2,32,256]{2,1,0:T(8,128)(2,1)S(1)} %slice.86), channel_id=1, source_target_pairs={{0,8},{1,9},{2,10},{3,11},{4,12},{5,13},{6,14},{7,15},{8,0},{9,1},... | collective-permute-start | bytes 98312 | tf_op jit(solution)/shard_map/ppermute | solution.py:428
  63.3 3.9 %weight_grads.8 = (bf16[32,64,5120]{2,1,0:T(8,128)(2,1)}, f32[32,5120]{1,0:T(8,128)}) custom-call(bf16[2048,256]{1,0:T(8,128)(2,1)S(1)} %get-tuple-element.50.hid_ref, bf16[256,5120]{1,0:T(8,128)(2,1)S(1)} %get-tuple-element.51.lagged_ref, f32[32,5120]{1,0:T(8,128)S(1)} %copy-done.1, ...), custom_call_target="tpu_custom_call", output_to_operand_aliasing={{0}: (4, {}), {1}: (5, {})} | custom-call | flops 1073741824 | bytes 8388608 | tf_op jit(solution)/shard_map/weight_grads/pallas_call | solution.py:256
  67.2 0.0 collective-permute-done.10
  67.2 2.4 %collective-permute-start.11 = (bf16[1,32,256]{2,1,0:T(8,128)(2,1)S(1)}, bf16[1,32,256]{2,1,0:T(8,128)(2,1)S(1)}, u32[]{:S(2)}, u32[]{:S(2)}) collective-permute-start(bf16[1,32,256]{2,1,0:T(8,128)(2,1)S(1)} %slice.87), channel_id=1, source_target_pairs={{0,16},{1,17},{2,18},{3,19},{4,20},{5,21},{6,22},{7,23},{8,24},{9,... | collective-permute-start | bytes 49160 | tf_op jit(solution)/shard_map/ppermute | solution.py:428
  69.6 3.9 %weight_grads.9 = (bf16[32,64,5120]{2,1,0:T(8,128)(2,1)}, f32[32,5120]{1,0:T(8,128)}) custom-call(bf16[2048,256]{1,0:T(8,128)(2,1)S(1)} %get-tuple-element.50.hid_ref, bf16[256,5120]{1,0:T(8,128)(2,1)S(1)} %get-tuple-element.51.lagged_ref, f32[32,5120]{1,0:T(8,128)S(1)} %copy-done.1, ...), custom_call_target="tpu_custom_call", output_to_operand_aliasing={{0}: (4, {}), {1}: (5, {})} | custom-call | flops 1073741824 | bytes 8388608 | tf_op jit(solution)/shard_map/weight_grads/pallas_call | solution.py:256
  73.5 0.0 collective-permute-done.11
  73.5 1.5 %collective-permute-start.13 = (f32[32,256]{1,0:T(8,128)S(1)}, f32[32,256]{1,0:T(8,128)S(1)}, u32[]{:S(2)}, u32[]{:S(2)}) collective-permute-start(f32[32,256]{1,0:T(8,128)S(1)} %fusion), channel_id=1, source_target_pairs={{0,1},{1,0},{2,3},{3,2},{4,5},{5,4},{6,7},{7,6},{8,9},{9,8},{10,11... | collective-permute-start | bytes 98312 | tf_op jit(solution)/shard_map/ppermute | solution.py:334
  75.0 3.5 %collective-permute-start.12 = (f32[32,256]{1,0:T(8,128)S(1)}, f32[32,256]{1,0:T(8,128)S(1)}, u32[]{:S(2)}, u32[]{:S(2)}) collective-permute-start(f32[32,256]{1,0:T(8,128)S(1)} %fusion), channel_id=1, source_target_pairs={{1,2},{2,1},{3,4},{4,3},{5,6},{6,5},{7,8},{8,7},{9,10},{10,9},{11,... | collective-permute-start | bytes 98312 | tf_op jit(solution)/shard_map/ppermute | solution.py:334
  78.6 1.4 %grad_dec.1 = f32[3,2048]{1,0:T(4,128)} custom-call(s32[1,2048]{1,0:T(1,128)S(1)} %bitcast.15, bf16[96,256]{1,0:T(8,128)(2,1)S(1)} %get-tuple-element.49.win_ref, f32[3,2048]{1,0:T(4,128)S(1)} %copy-done.2, bf16[3,256,2048]{2,1,0:T(8,128)(2,1)S(1)} %bitcast.12), custom_call_target="tpu_custom_call" | custom-call | flops 603979776 | bytes 3145728 | tf_op jit(solution)/shard_map/grad_dec/pallas_call | solution.py:315
  80.0 0.0 collective-permute-done.13
  80.0 0.3 collective-permute-done.12
  80.3 1.8 %grad_enc.1 = f32[3,2048]{1,0:T(4,128)} custom-call(s32[1,2048]{1,0:T(1,128)S(1)} %bitcast.16, f32[96,256]{1,0:T(8,128)S(1)} %pad_maximum_fusion.1.grad_ref, bf16[3,256,2048]{2,1,0:T(8,128)(2,1)S(1)} %bitcast.13), custom_call_target="tpu_custom_call" | custom-call | flops 603979776 | bytes 3145728 | tf_op jit(solution)/shard_map/grad_enc/pallas_call | solution.py:315
  (34 shorter events, 0.3 us)
Async XLA Ops:
  0.6 2.4 %copy-start.7 = (s32[2048]{0:T(1024)S(1)}, s32[2048]{0:T(1024)}, u32[]{:S(2)}) copy-start(s32[2048]{0:T(1024)} %param.10) | copy-start | bytes 24580
  0.6 2.4 %copy-start.2 = (f32[3,2048]{1,0:T(4,128)S(1)}, f32[3,2048]{1,0:T(4,128)}, u32[]{:S(2)}) copy-start(f32[3,2048]{1,0:T(4,128)} %dec_ref.3) | copy-start | bytes 73732
  0.7 2.4 %copy-start.3 = (f32[3,2048]{1,0:T(4,128)S(1)}, f32[3,2048]{1,0:T(4,128)}, u32[]{:S(2)}) copy-start(f32[3,2048]{1,0:T(4,128)} %enc_ref.1) | copy-start | bytes 73732
  3.0 11.9 %copy-start = (bf16[32,64,5120]{2,1,0:T(8,128)(2,1)S(1)}, bf16[32,64,5120]{2,1,0:T(8,128)(2,1)}, u32[]{:S(2)}) copy-start(bf16[32,64,5120]{2,1,0:T(8,128)(2,1)} %weight_ref.17) | copy-start | bytes 62914564
  3.0 11.9 %copy-start.1 = (f32[32,5120]{1,0:T(8,128)S(1)}, f32[32,5120]{1,0:T(8,128)}, u32[]{:S(2)}) copy-start(f32[32,5120]{1,0:T(8,128)} %logit_ref.13) | copy-start | bytes 1966084
  4.8 5.0 %collective-permute-start = (f32[32,256]{1,0:T(8,128)S(1)}, f32[32,256]{1,0:T(8,128)S(1)}, u32[]{:S(2)}, u32[]{:S(2)}) collective-permute-start(f32[32,256]{1,0:T(8,128)S(1)} %get-tuple-element.67), channel_id=1, source_target_pairs={{0,1},{1,0},{2,3},{3,2},{4,5},{5,4},{6,7},{7,6},{8,9},{9,8},{10,11... | collective-permute-start | bytes 98312 | tf_op jit(solution)/shard_map/ppermute | solution.py:334
  6.9 5.6 %collective-permute-start.1 = (f32[32,256]{1,0:T(8,128)S(1)}, f32[32,256]{1,0:T(8,128)S(1)}, u32[]{:S(2)}, u32[]{:S(2)}) collective-permute-start(f32[32,256]{1,0:T(8,128)S(1)} %get-tuple-element.68), channel_id=1, source_target_pairs={{1,2},{2,1},{3,4},{4,3},{5,6},{6,5},{7,8},{8,7},{9,10},{10,9},{11,... | collective-permute-start | bytes 98312 | tf_op jit(solution)/shard_map/ppermute | solution.py:334
  12.6 3.6 %collective-permute-start.2 = (bf16[1,32,256]{2,1,0:T(8,128)(2,1)S(1)}, bf16[1,32,256]{2,1,0:T(8,128)(2,1)S(1)}, u32[]{:S(2)}, u32[]{:S(2)}) collective-permute-start(bf16[1,32,256]{2,1,0:T(8,128)(2,1)S(1)} %get-tuple-element.63), channel_id=1, source_target_pairs={{0,16},{1,17},{2,18},{3,19},{4,20},{5,21},{6,22},{7,23},{8,24},{9,... | collective-permute-start | bytes 49160 | tf_op jit(solution)/shard_map/ppermute | solution.py:397
  16.1 3.0 %collective-permute-start.3 = (bf16[2,32,256]{2,1,0:T(8,128)(2,1)S(1)}, bf16[2,32,256]{2,1,0:T(8,128)(2,1)S(1)}, u32[]{:S(2)}, u32[]{:S(2)}) collective-permute-start(bf16[2,32,256]{2,1,0:T(8,128)(2,1)S(1)} %pad_maximum_fusion.3), channel_id=1, source_target_pairs={{0,8},{1,9},{2,10},{3,11},{4,12},{5,13},{6,14},{7,15},{8,0},{9,1},... | collective-permute-start | bytes 98312 | tf_op jit(solution)/shard_map/ppermute | solution.py:397
  19.2 3.2 %collective-permute-start.4 = (bf16[4,32,256]{2,1,0:T(8,128)(2,1)S(1)}, bf16[4,32,256]{2,1,0:T(8,128)(2,1)S(1)}, u32[]{:S(2)}, u32[]{:S(2)}) collective-permute-start(bf16[4,32,256]{2,1,0:T(8,128)(2,1)S(1)} %pad_maximum_fusion.2), channel_id=1, source_target_pairs={{0,4},{1,5},{2,6},{3,7},{4,0},{5,1},{6,2},{7,3},{8,12},{9,13},{10,... | collective-permute-start | bytes 196616 | tf_op jit(solution)/shard_map/ppermute | solution.py:397
  22.4 4.6 %collective-permute-start.5 = (bf16[8,32,256]{2,1,0:T(8,128)(2,1)S(1)}, bf16[8,32,256]{2,1,0:T(8,128)(2,1)S(1)}, u32[]{:S(2)}, u32[]{:S(2)}) collective-permute-start(bf16[8,32,256]{2,1,0:T(8,128)(2,1)S(1)} %pad_maximum_fusion), channel_id=1, source_target_pairs={{0,1},{1,0},{2,3},{3,2},{4,5},{5,4},{6,7},{7,6},{8,9},{9,8},{10,11... | collective-permute-start | bytes 393224 | tf_op jit(solution)/shard_map/ppermute | solution.py:397
  24.3 10.0 %copy-start.4 = (f32[32,64]{1,0:T(8,128)S(1)}, f32[32,64]{1,0:T(8,128)}, u32[]{:S(2)}) copy-start(f32[32,64]{1,0:T(8,128)} %bias_ref.1) | copy-start | bytes 24580
  24.3 10.0 %copy-start.5 = (f32[32,64]{1,0:T(8,128)S(1)}, f32[32,64]{1,0:T(8,128)}, u32[]{:S(2)}) copy-start(f32[32,64]{1,0:T(8,128)} %out_w_ref.1) | copy-start | bytes 24580
  24.3 10.0 %copy-start.6 = (f32[32]{0:T(128)S(1)}, f32[32]{0:T(128)}, u32[]{:S(2)}) copy-start(f32[32]{0:T(128)} %param.17) | copy-start | bytes 388
  27.0 7.3 %collective-permute-start.6 = (bf16[16,32,256]{2,1,0:T(8,128)(2,1)S(1)}, bf16[16,32,256]{2,1,0:T(8,128)(2,1)S(1)}, u32[]{:S(2)}, u32[]{:S(2)}) collective-permute-start(bf16[16,32,256]{2,1,0:T(8,128)(2,1)S(1)} %get-tuple-element.65), channel_id=1, source_target_pairs={{0,2},{1,3},{2,0},{3,1},{4,6},{5,7},{6,4},{7,5},{8,10},{9,11},{10,... | collective-permute-start | bytes 786440 | tf_op jit(solution)/shard_map/ppermute | solution.py:397
  47.8 1.6 %collective-permute-start.7 = (bf16[16,32,256]{2,1,0:T(8,128)(2,1)S(1)}, bf16[16,32,256]{2,1,0:T(8,128)(2,1)S(1)}, u32[]{:S(2)}, u32[]{:S(2)}) collective-permute-start(bf16[16,32,256]{2,1,0:T(8,128)(2,1)S(1)} %slice.83), channel_id=1, source_target_pairs={{0,2},{1,3},{2,0},{3,1},{4,6},{5,7},{6,4},{7,5},{8,10},{9,11},{10,... | collective-permute-start | bytes 786440 | tf_op jit(solution)/shard_map/ppermute | solution.py:428
  49.5 7.9 %collective-permute-start.8 = (bf16[8,32,256]{2,1,0:T(8,128)(2,1)S(1)}, bf16[8,32,256]{2,1,0:T(8,128)(2,1)S(1)}, u32[]{:S(2)}, u32[]{:S(2)}) collective-permute-start(bf16[8,32,256]{2,1,0:T(8,128)(2,1)S(1)} %slice.84), channel_id=1, source_target_pairs={{0,1},{1,0},{2,3},{3,2},{4,5},{5,4},{6,7},{7,6},{8,9},{9,8},{10,11... | collective-permute-start | bytes 393224 | tf_op jit(solution)/shard_map/ppermute | solution.py:428
  57.4 4.5 %collective-permute-start.9 = (bf16[4,32,256]{2,1,0:T(8,128)(2,1)S(1)}, bf16[4,32,256]{2,1,0:T(8,128)(2,1)S(1)}, u32[]{:S(2)}, u32[]{:S(2)}) collective-permute-start(bf16[4,32,256]{2,1,0:T(8,128)(2,1)S(1)} %slice.85), channel_id=1, source_target_pairs={{0,4},{1,5},{2,6},{3,7},{4,0},{5,1},{6,2},{7,3},{8,12},{9,13},{10,... | collective-permute-start | bytes 196616 | tf_op jit(solution)/shard_map/ppermute | solution.py:428
  61.9 5.2 %collective-permute-start.10 = (bf16[2,32,256]{2,1,0:T(8,128)(2,1)S(1)}, bf16[2,32,256]{2,1,0:T(8,128)(2,1)S(1)}, u32[]{:S(2)}, u32[]{:S(2)}) collective-permute-start(bf16[2,32,256]{2,1,0:T(8,128)(2,1)S(1)} %slice.86), channel_id=1, source_target_pairs={{0,8},{1,9},{2,10},{3,11},{4,12},{5,13},{6,14},{7,15},{8,0},{9,1},... | collective-permute-start | bytes 98312 | tf_op jit(solution)/shard_map/ppermute | solution.py:428
  67.2 6.3 %collective-permute-start.11 = (bf16[1,32,256]{2,1,0:T(8,128)(2,1)S(1)}, bf16[1,32,256]{2,1,0:T(8,128)(2,1)S(1)}, u32[]{:S(2)}, u32[]{:S(2)}) collective-permute-start(bf16[1,32,256]{2,1,0:T(8,128)(2,1)S(1)} %slice.87), channel_id=1, source_target_pairs={{0,16},{1,17},{2,18},{3,19},{4,20},{5,21},{6,22},{7,23},{8,24},{9,... | collective-permute-start | bytes 49160 | tf_op jit(solution)/shard_map/ppermute | solution.py:428
  73.5 6.4 %collective-permute-start.13 = (f32[32,256]{1,0:T(8,128)S(1)}, f32[32,256]{1,0:T(8,128)S(1)}, u32[]{:S(2)}, u32[]{:S(2)}) collective-permute-start(f32[32,256]{1,0:T(8,128)S(1)} %fusion), channel_id=1, source_target_pairs={{0,1},{1,0},{2,3},{3,2},{4,5},{5,4},{6,7},{7,6},{8,9},{9,8},{10,11... | collective-permute-start | bytes 98312 | tf_op jit(solution)/shard_map/ppermute | solution.py:334
  75.0 5.2 %collective-permute-start.12 = (f32[32,256]{1,0:T(8,128)S(1)}, f32[32,256]{1,0:T(8,128)S(1)}, u32[]{:S(2)}, u32[]{:S(2)}) collective-permute-start(f32[32,256]{1,0:T(8,128)S(1)} %fusion), channel_id=1, source_target_pairs={{1,2},{2,1},{3,4},{4,3},{5,6},{6,5},{7,8},{8,7},{9,10},{10,9},{11,... | collective-permute-start | bytes 98312 | tf_op jit(solution)/shard_map/ppermute | solution.py:334

commit v2 on v1

--- a/solution.py
+++ b/solution.py
@@ -108,26 +108,28 @@
     return in_vmem(out)
 
 
-def transition_kernel(steps, norm, order, inverse, parts, device_ref, lat_ref, own_ref, bias_ref,
+def transition_kernel(steps, norm, core, order, inverse, parts, device_ref, lat_ref, own_ref, bias_ref,
                       out_w_ref, var_ref, dec_ref, sq_ref, *refs):
     eff = refs[:parts]
-    hid_out, lagged_out, grad_out, direct_out, window_out, lagged, pre, hid_t, folded = refs[parts:]
+    hid_out, lagged_out, grad_out, direct_out, window_out, lagged, work, hid_t, folded = refs[parts:]
     blocks, size, rows = lat_ref.shape
     latents = blocks * size
     span, lag_width = eff[0].shape
     lat_dev, hidden = bias_ref.shape
     group = span // hidden
     device = device_ref[0]
-
-    def spot(block):
+    side = (device >> core) & 1
+
+    def spot(owner):
+        away = owner ^ device
         found = jnp.int32(0)
-        for bit, moved in inverse:
-            found = found | (((block >> bit) & 1) << moved)
+        for bit, first, second in inverse:
+            found = found | (((away >> bit) & 1) << jnp.where((owner >> core) & 1, second, first))
         return found
 
     for p in range(blocks):
         values = lat_ref[p].astype(f32)
-        at = pl.multiple_of((device ^ order[p]) * size, size) if blocks > 1 else 0
+        at = pl.multiple_of((device ^ jnp.where(side, order[1][p], order[0][p])) * size, size)
         for lag in range(1, LAGS + 1):
             turned = pltpu.roll(values, lag, 1).astype(bf16)
             lagged[pl.ds((lag - 1) * latents + at, size), :] = turned
@@ -136,6 +138,7 @@
     column = lax.broadcasted_iota(jnp.int32, (group, rows), 1)
     valid = lax.rem(column, steps) >= LAGS
     for part in range(parts):
+        pre = work.at[part % 2]
         pre[...] = jnp.dot(eff[part][...], lagged[...], preferred_element_type=f32)
         first = part * group
         for k in range(group):
@@ -174,13 +177,11 @@
     if blocks == 1:
         grad_out[0] = total
         return
-    here = spot(device)
     for block in range(blocks):
-        at = sum(((block >> bit) & 1) << moved for bit, moved in inverse)
-        grad_out[at ^ here] = total[block * size : (block + 1) * size]
+        grad_out[spot(jnp.int32(block))] = total[block * size : (block + 1) * size]
     grad_out[0] += direct_out[...]
-    below = spot(jnp.maximum(device - 1, 0)) ^ here
-    above = spot(jnp.minimum(device + 1, blocks - 1)) ^ here
+    below = spot(jnp.maximum(device - 1, 0))
+    above = spot(jnp.minimum(device + 1, blocks - 1))
     for n, at in ((0, below), (1, 0), (2, above)):
         part = slice(n * size, (n + 1) * size)
         values = lat_ref[at]
@@ -188,14 +189,14 @@
         grad_out[at] += norm * (values.astype(f32) * sq_ref[part, :] - dec_ref[part, :])
 
 
-def transition(steps, norm, order, inverse, device, lat3, own, bias, out_w, var, dec_sums, squares, eff):
+def transition(steps, norm, core, order, inverse, device, lat3, own, bias, out_w, var, dec_sums, squares, eff):
     blocks, size, rows = lat3.shape
     lat_dev, hidden = bias.shape
     span, lag_width = eff[0].shape
     km = lat_dev * hidden
     shape = jax.ShapeDtypeStruct
     return pl.pallas_call(
-        functools.partial(transition_kernel, steps, norm, order, inverse, len(eff)),
+        functools.partial(transition_kernel, steps, norm, core, order, inverse, len(eff)),
         in_specs=[pl.BlockSpec(memory_space=pltpu.SMEM)] + [VMEM] * (7 + len(eff)),
         out_specs=[VMEM] * 5,
         out_shape=[
@@ -207,7 +208,7 @@
         ],
         scratch_shapes=[
             pltpu.VMEM((lag_width, rows), bf16),
-            pltpu.VMEM((span, rows), f32),
+            pltpu.VMEM((2, span, rows), f32),
             pltpu.VMEM((rows, km), bf16),
             pltpu.VMEM((rows, blocks * size), f32),
         ],
@@ -224,7 +225,7 @@
 def weight_kernel(start, hid_ref, lagged_ref, logit_ref, weight_ref, *refs):
     trans_out, graph_out, work = refs[-3:]
     lat_dev, hidden, lag_width = weight_ref.shape
-    tile = lagged_ref.shape[1]
+    tile = graph_out.shape[1]
     group = group_of(lat_dev)
     at = pl.multiple_of(start + pl.program_id(0) * tile, tile)
     for g in range(lat_dev // group):
@@ -234,15 +235,16 @@
             lagged_ref[...],
             preferred_element_type=f32,
         )
+        latents = slice(g * group, (g + 1) * group)
+        edge = jax.nn.sigmoid(logit_ref[latents, :])
         for k in range(group):
             n = g * group + k
-            edge = jax.nn.sigmoid(logit_ref[n : n + 1, :])
             grad = held[k * hidden : (k + 1) * hidden, :]
-            trans_out[n] = (grad * edge).astype(bf16)
-            flip = edge * (1.0 - edge)
+            trans_out[n] = (grad * edge[k : k + 1]).astype(bf16)
             value = weight_ref[n, :, pl.ds(at, tile)].astype(f32)
-            total = jnp.sum(grad * value, axis=0, keepdims=True)
-            graph_out[n : n + 1, :] = total * flip + sparsity_weight * flip
+            graph_out[n : n + 1, :] = jnp.sum(grad * value, axis=0, keepdims=True)
+        flip = edge * (1.0 - edge)
+        graph_out[latents, :] = graph_out[latents, :] * flip + sparsity_weight * flip
 
 
 def weight_grads(hid, lagged, logits, weights, first, count, held):
@@ -278,7 +280,7 @@
     )(hid, lagged, logits, weights, *held)
 
 
-TILE = 256
+TILE = 512
 
 
 def pick(mask, table, fields):
@@ -302,12 +304,13 @@
 
 
 def grad_enc_kernel(loc_ref, grad_ref, fields_ref, out_ref):
-    high, low = (part.astype(bf16) for part in pieces(grad_ref[...], 2))
-    mask = mask_of(loc_ref, high.shape[0])
+    width = grad_ref.shape[0]
+    both = jnp.concatenate([part.astype(bf16) for part in pieces(grad_ref[...], 2)], axis=0)
+    mask = mask_of(loc_ref, width)
     for var in range(fields_ref.shape[0]):
-        out_ref[var : var + 1, :] = pick(mask, high, fields_ref[var]) + pick(
-            mask, low, fields_ref[var]
-        )
+        sums = jnp.dot(both, fields_ref[var], preferred_element_type=f32)
+        sums = jnp.where(mask, sums[:width] + sums[width:], 0.0)
+        out_ref[var : var + 1, :] = jnp.sum(sums, axis=0, keepdims=True)
 
 
 def cell_call(kernel, loc, table, extras, fields3, name):
@@ -362,9 +365,12 @@
     count = space * lat
     device = lax.axis_index(AXES)
     doubling = count & (count - 1) == 0 and lat_dev % 16 == 0
-    bits = [n for n in range(count.bit_length() - 2, -1, -1)]
     core = lat.bit_length() - 1
-    bits = [n for n in bits if n != core] + [core]
+    bits = [n for n in range(count.bit_length() - 2, -1, -1) if n != core]
+    bits = list(zip(bits, bits[:-2] + bits[-2:][::-1])) + [(core, core)]
+
+    def swap(pair):
+        return [(n, n ^ (1 << pair[(n >> core) & 1])) for n in range(count)]
 
     loc = (cell_latent - (device - 1) * lat_dev)[None]
     fields3 = jnp.transpose(fields.reshape(rows, var_count, cell_count), (1, 0, 2))
@@ -392,16 +398,22 @@
 
     if doubling:
         gathered = own_bf[None]
-        for bit in bits:
-            route = [(n, n ^ (1 << bit)) for n in range(count)]
-            got = beside(lax.ppermute(gathered, AXES, route), gathered)
+        for choice in bits:
+            got = beside(lax.ppermute(gathered, AXES, swap(choice)), gathered)
             gathered = jnp.concatenate([gathered, got], axis=0)
-        order = [0]
-        for bit in bits:
-            order = order + [n ^ (1 << bit) for n in order]
-        inverse = [(bit, n) for n, bit in enumerate(bits)]
+        order = [[0], [0]]
+        for pair in bits:
+            came = order if pair[0] != core else order[::-1]
+            order = [
+                own_order + [n ^ (1 << bit) for n in other]
+                for own_order, other, bit in zip(order, came, pair)
+            ]
+        inverse = [
+            (bit, [pair[0] for pair in bits].index(bit), [pair[1] for pair in bits].index(bit))
+            for bit, _ in bits
+        ]
     else:
-        order, inverse = [0], []
+        order, inverse = [[0], [0]], []
         gathered = lax.all_gather(own_bf, AXES, axis=0, tiled=True)
         padded = jnp.pad(gathered, ((lat_dev, lat_dev), (0, 0)))
         window = lax.dynamic_slice_in_dim(padded, device * lat_dev, width, 0)
@@ -411,31 +423,42 @@
         gathered = beside(gathered, enc_sums)
     eff = [in_vmem(part) for part in eff]
     hid, lagged, partial, direct, seen = transition(
-        step_count, norm, order, inverse, device.astype(jnp.int32)[None], gathered, own,
+        step_count, norm, core, order, inverse, device.astype(jnp.int32)[None], gathered, own,
         hidden_bias, out_weight, noise_var[None], dec_sums, squares, eff,
     )
     window = seen if doubling else window
 
+    def decoder(values):
+        kernel = functools.partial(grad_dec_kernel, norm)
+        return cell_call(kernel, loc, values, [dec_weight], fields3, "grad_dec")
+
     if doubling:
-        held = []
-        total = partial
-        fillers = LAGS if lag_width // LAGS % 256 == 0 else 1
-        chunk = lag_width // fillers
-        done = 0
-        for n, bit in enumerate(reversed(bits)):
+        held, total, done = [], partial, 0
+        tiles = lag_width // TILE
+        last = tiles // 5
+        shares = {1: tiles - 3 * last, 2: last, 3: last}
+
+        def weight_share(n, held, done):
+            return weight_grads(
+                hid, lagged, graph_logits, held_weights, done * TILE, n * TILE, held
+            )
+
+        for n, pair in enumerate(reversed(bits)):
             half = total.shape[0] // 2
-            route = [(m, m ^ (1 << bit)) for m in range(count)]
-            got = lax.ppermute(total[half:].astype(bf16), AXES, route)
-            if done < fillers:
-                held = weight_grads(
-                    hid, lagged, graph_logits, held_weights, done * chunk, chunk, held
-                )
-                done += 1
+            got = lax.ppermute(total[half:].astype(bf16), AXES, swap(pair))
+            if n in shares:
+                held = weight_share(shares[n], held, done)
+                done += shares[n]
+                got, held = lax.optimization_barrier((got, held))
+            elif n == 4:
+                seen, _ = lax.optimization_barrier((window, total))
+                got, grad_dec = lax.optimization_barrier((got, decoder(seen)))
             total = total[:half] + got.astype(f32)
-        while done < fillers:
-            held = weight_grads(hid, lagged, graph_logits, held_weights, done * chunk, chunk, held)
-            done += 1
         own_grad = total[0]
+        hid, own_grad = lax.optimization_barrier((hid, own_grad))
+        first, second, even = from_neighbours(own_grad, own_grad, device, count)
+        held = weight_share(tiles - done, held, done)
+        first, second, held = lax.optimization_barrier((first, second, held))
         grad_trans, grad_graph = held
     else:
         grad_trans, grad_graph = weight_grads(
@@ -447,11 +470,9 @@
         table = lax.dynamic_update_slice_in_dim(table, extra, device * lat_dev, 0)
         partial = partial[0] + table[lat_dev : lat_dev + latent_count]
         own_grad = lax.psum_scatter(partial, AXES, scatter_dimension=0, tiled=True)
-
-    grad_dec = cell_call(
-        functools.partial(grad_dec_kernel, norm), loc, window, [dec_weight], fields3, "grad_dec"
-    )
-    first, second, even = from_neighbours(own_grad, own_grad, device, count)
+        grad_dec = decoder(window)
+        first, second, even = from_neighbours(own_grad, own_grad, device, count)
+
     grad_window = jnp.concatenate(
         [jnp.where(even, second, first), own_grad, jnp.where(even, first, second)], axis=0
     )

time: 83.3 us -> 79.5 us (0.954)
  Pallas kernels: 41.6 us -> 37.8 us
  starting transfers between devices: 27.7 us -> 29.2 us
    pallas_call x5 -> x4, Pallas kernels: 19.4 us -> 15.9 us  [weight_grads(): pl.pallas_call(functools.partial(weight_kernel, first), grid=(count // ti...]
    ppermute x10, starting transfers between devices: 17.7 us -> 18.7 us  [the longest x5 13.3 us: body(): got = beside(lax.ppermute(gathered, AXES, swap(choice)), gathered)]
  transfers between devices with their start and end apart: 14 -> 14, of which waited for: 8 -> 7; matrix products, arithmetic and copies ran while one was open for 0% -> 0% of each run, Pallas kernels for 30% -> 27%
where the time goes in v2:
time: 79.5 us; the launch traced here: 79 us
  Pallas kernels  37.8 us (48%)
  starting transfers between devices  29.2 us (37%)
  waiting for transfers between devices  8.58 us (11%)
  local copies, waits for them, and re-layouts  2.28 us (3%)
  between operations  0.95 us (1%)
    pallas_call x4, Pallas kernels, weight_grads(): pl.pallas_call(functools.partial(weight_kernel, first), grid=(count // ti...  15.9 us
    pallas_call x1, Pallas kernels, transition(): pl.pallas_call(functools.partial(transition_kernel, steps, norm, core, or...  13.5 us
    ppermute x5, starting transfers between devices, body(): got = beside(lax.ppermute(gathered, AXES, swap(choice)), gathered)  13.3 us
    ppermute x4, starting transfers between devices, paired(): return lax.ppermute(block, AXES, route)  10.5 us
    ppermute x5, starting transfers between devices, body(): got = lax.ppermute(total[half:].astype(bf16), AXES, swap(pair))  5.45 us
    ppermute x5, waiting for transfers between devices, body(): got = beside(lax.ppermute(gathered, AXES, swap(choice)), gathered)  4.67 us
    pallas_call x4, Pallas kernels, effective(): pl.pallas_call(functools.partial(edge_kernel, group, part * group), in_sp...  3.71 us
    pallas_call x2, Pallas kernels, cell_call(): pl.pallas_call(kernel, in_specs=[VMEM] * (3 + len(extras)), out_specs=VME...  2.87 us
  transfers between devices with their start and end apart: 14, of which 7 were waited for; matrix products, arithmetic and copies ran while one was open for 0% of the time, Pallas kernels for 27%

profile of v2, /device:TPU:1, one launch (start us, length us, event | category | flops | bytes accessed | tf_op | source)
XLA Modules:
  0.0 79.0 jit_solution(5031635597842610916)
XLA Ops:
  0.7 2.1 %copy.19 = bf16[4,64,3,2048]{3,1,0,2:T(8,128)(2,1)S(1)} copy(bf16[4,64,3,2048]{3,1,2,0:T(8,128)(2,1)} %param.9) | data formatting | bytes 6291456 | tf_op args[0]
  2.8 0.0 copy-start
  2.8 0.0 copy-start.1
  2.9 1.7 %encode.1 = (f32[96,256]{1,0:T(8,128)S(1)}, f32[96,256]{1,0:T(8,128)S(1)}, f32[96,256]{1,0:T(8,128)S(1)}) custom-call(s32[1,2048]{1,0:T(1,128)S(1)} %bitcast.14, f32[3,2048]{1,0:T(4,128)S(1)} %copy-done.3, f32[3,2048]{1,0:T(4,128)S(1)} %copy-done.2, bf16[3,256,2048]{2,1,0:T(8,128)(2,1)S(1)} %bitcast.11), custom_call_target="tpu_custom_call" | custom-call | flops 7549747200 | bytes 3145728 | tf_op jit(solution)/shard_map/encode/pallas_call | solution.py:68
  4.6 2.1 %collective-permute-start = (f32[32,256]{1,0:T(8,128)S(1)}, f32[32,256]{1,0:T(8,128)S(1)}, u32[]{:S(2)}, u32[]{:S(2)}) collective-permute-start(f32[32,256]{1,0:T(8,128)S(1)} %get-tuple-element.99), channel_id=1, source_target_pairs={{0,1},{1,0},{2,3},{3,2},{4,5},{5,4},{6,7},{7,6},{8,9},{9,8},{10,11... | collective-permute-start | bytes 98312 | tf_op jit(solution)/shard_map/ppermute | solution.py:337
  6.7 2.9 %collective-permute-start.1 = (f32[32,256]{1,0:T(8,128)S(1)}, f32[32,256]{1,0:T(8,128)S(1)}, u32[]{:S(2)}, u32[]{:S(2)}) collective-permute-start(f32[32,256]{1,0:T(8,128)S(1)} %get-tuple-element.100), channel_id=1, source_target_pairs={{1,2},{2,1},{3,4},{4,3},{5,6},{6,5},{7,8},{8,7},{9,10},{10,9},{11,... | collective-permute-start | bytes 98312 | tf_op jit(solution)/shard_map/ppermute | solution.py:337
  9.6 0.0 collective-permute-done
  9.6 2.7 %collective-permute-done.1 = f32[32,256]{1,0:T(8,128)S(1)} collective-permute-done((f32[32,256]{1,0:T(8,128)S(1)}, f32[32,256]{1,0:T(8,128)S(1)}, u32[]{:S(2)}, u32[]{:S(2)}) %collective-permute-start.1) | collective-permute-done | bytes 32800 | tf_op jit(solution)/shard_map/ppermute | solution.py:337
  12.4 2.4 %collective-permute-start.2 = (bf16[1,32,256]{2,1,0:T(8,128)(2,1)S(1)}, bf16[1,32,256]{2,1,0:T(8,128)(2,1)S(1)}, u32[]{:S(2)}, u32[]{:S(2)}) collective-permute-start(bf16[1,32,256]{2,1,0:T(8,128)(2,1)S(1)} %get-tuple-element.95), channel_id=1, source_target_pairs={{0,16},{1,17},{2,18},{3,19},{4,20},{5,21},{6,22},{7,23},{8,24},{9,... | collective-permute-start | bytes 49160 | tf_op jit(solution)/shard_map/ppermute | solution.py:402
  14.7 0.0 copy-done
  14.7 0.9 %effective.4.refs_0_ = bf16[512,5120]{1,0:T(8,128)(2,1)S(1)} custom-call(f32[32,5120]{1,0:T(8,128)S(1)} %copy-done.1, bf16[32,64,5120]{2,1,0:T(8,128)(2,1)S(1)} %copy-done), custom_call_target="tpu_custom_call" | custom-call | flops 5242880 | bytes 10485760 | tf_op jit(solution)/shard_map/effective/pallas_call | solution.py:95
  15.7 0.2 collective-permute-done.2
  15.9 1.3 %collective-permute-start.3 = (bf16[2,32,256]{2,1,0:T(8,128)(2,1)S(1)}, bf16[2,32,256]{2,1,0:T(8,128)(2,1)S(1)}, u32[]{:S(2)}, u32[]{:S(2)}) collective-permute-start(bf16[2,32,256]{2,1,0:T(8,128)(2,1)S(1)} %pad_maximum_fusion.3), channel_id=1, source_target_pairs={{0,8},{1,9},{2,10},{3,11},{4,12},{5,13},{6,14},{7,15},{8,0},{9,1},... | collective-permute-start | bytes 98312 | tf_op jit(solution)/shard_map/ppermute | solution.py:402
  17.2 0.9 %effective.5.refs_1_ = bf16[512,5120]{1,0:T(8,128)(2,1)S(1)} custom-call(f32[32,5120]{1,0:T(8,128)S(1)} %copy-done.1, bf16[32,64,5120]{2,1,0:T(8,128)(2,1)S(1)} %copy-done), custom_call_target="tpu_custom_call" | custom-call | flops 5242880 | bytes 10485760 | tf_op jit(solution)/shard_map/effective/pallas_call | solution.py:95
  18.2 0.8 %collective-permute-done.3 = bf16[2,32,256]{2,1,0:T(8,128)(2,1)S(1)} collective-permute-done((bf16[2,32,256]{2,1,0:T(8,128)(2,1)S(1)}, bf16[2,32,256]{2,1,0:T(8,128)(2,1)S(1)}, u32[]{:S(2)}, u32[]{:S(2)}) %collective-permute-start.3) | collective-permute-done | bytes 32800 | tf_op jit(solution)/shard_map/ppermute | solution.py:402
  19.0 1.6 %collective-permute-start.4 = (bf16[4,32,256]{2,1,0:T(8,128)(2,1)S(1)}, bf16[4,32,256]{2,1,0:T(8,128)(2,1)S(1)}, u32[]{:S(2)}, u32[]{:S(2)}) collective-permute-start(bf16[4,32,256]{2,1,0:T(8,128)(2,1)S(1)} %pad_maximum_fusion.2), channel_id=1, source_target_pairs={{0,4},{1,5},{2,3},{3,2},{4,0},{5,1},{6,7},{7,6},{8,12},{9,13},{10,... | collective-permute-start | bytes 196616 | tf_op jit(solution)/shard_map/ppermute | solution.py:402
  20.6 0.9 %effective.6.refs_2_ = bf16[512,5120]{1,0:T(8,128)(2,1)S(1)} custom-call(f32[32,5120]{1,0:T(8,128)S(1)} %copy-done.1, bf16[32,64,5120]{2,1,0:T(8,128)(2,1)S(1)} %copy-done), custom_call_target="tpu_custom_call" | custom-call | flops 5242880 | bytes 10485760 | tf_op jit(solution)/shard_map/effective/pallas_call | solution.py:95
  21.5 0.7 collective-permute-done.4
  22.3 1.8 %collective-permute-start.5 = (bf16[8,32,256]{2,1,0:T(8,128)(2,1)S(1)}, bf16[8,32,256]{2,1,0:T(8,128)(2,1)S(1)}, u32[]{:S(2)}, u32[]{:S(2)}) collective-permute-start(bf16[8,32,256]{2,1,0:T(8,128)(2,1)S(1)} %pad_maximum_fusion), channel_id=1, source_target_pairs={{0,1},{1,0},{2,6},{3,7},{4,5},{5,4},{6,2},{7,3},{8,9},{9,8},{10,14... | collective-permute-start | bytes 393224 | tf_op jit(solution)/shard_map/ppermute | solution.py:402
  24.1 0.0 copy-start.6
  24.1 0.9 %effective.7.refs_3_ = bf16[512,5120]{1,0:T(8,128)(2,1)S(1)} custom-call(f32[32,5120]{1,0:T(8,128)S(1)} %copy-done.1, bf16[32,64,5120]{2,1,0:T(8,128)(2,1)S(1)} %copy-done), custom_call_target="tpu_custom_call" | custom-call | flops 5242880 | bytes 10485760 | tf_op jit(solution)/shard_map/effective/pallas_call | solution.py:95
  25.1 1.7 %collective-permute-done.5 = bf16[8,32,256]{2,1,0:T(8,128)(2,1)S(1)} collective-permute-done((bf16[8,32,256]{2,1,0:T(8,128)(2,1)S(1)}, bf16[8,32,256]{2,1,0:T(8,128)(2,1)S(1)}, u32[]{:S(2)}, u32[]{:S(2)}) %collective-permute-start.5) | collective-permute-done | bytes 131104 | tf_op jit(solution)/shard_map/ppermute | solution.py:402
  26.8 6.1 %collective-permute-start.6 = (bf16[16,32,256]{2,1,0:T(8,128)(2,1)S(1)}, bf16[16,32,256]{2,1,0:T(8,128)(2,1)S(1)}, u32[]{:S(2)}, u32[]{:S(2)}) collective-permute-start(bf16[16,32,256]{2,1,0:T(8,128)(2,1)S(1)} %get-tuple-element.97), channel_id=1, source_target_pairs={{0,2},{1,3},{2,0},{3,1},{4,6},{5,7},{6,4},{7,5},{8,10},{9,11},{10,... | collective-permute-start | bytes 786440 | tf_op jit(solution)/shard_map/ppermute | solution.py:402
  33.0 1.2 %collective-permute-done.6 = bf16[16,32,256]{2,1,0:T(8,128)(2,1)S(1)} collective-permute-done((bf16[16,32,256]{2,1,0:T(8,128)(2,1)S(1)}, bf16[16,32,256]{2,1,0:T(8,128)(2,1)S(1)}, u32[]{:S(2)}, u32[]{:S(2)}) %collective-permute-start.6) | collective-permute-done | bytes 262176 | tf_op jit(solution)/shard_map/ppermute | solution.py:402
  34.2 0.0 copy-done.4
  34.2 0.0 copy-done.5
  34.2 13.5 %transition.1 = (bf16[2048,256]{1,0:T(8,128)(2,1)S(1)}, bf16[256,5120]{1,0:T(8,128)(2,1)S(1)}, f32[32,32,256]{2,1,0:T(8,128)S(1)}, f32[32,256]{1,0:T(8,128)}, bf16[96,256]{1,0:T(8,128)(2,1)S(1)}) custom-call(s32[1]{0:T(128)} %bitcast.1.device_ref, bf16[32,32,256]{2,1,0:T(8,128)(2,1)S(1)} %constant_dynamic-update-slice_fusion.5.lat_ref, ...), custom_call_target="tpu_custom_call" | custom-call | flops 10737418240 | bytes 20971520 | tf_op jit(solution)/shard_map/transition/pallas_call | solution.py:198
  47.8 0.4 collective-permute-start.7
  48.2 1.2 %collective-permute-done.7 = bf16[16,32,256]{2,1,0:T(8,128)(2,1)S(1)} collective-permute-done((bf16[16,32,256]{2,1,0:T(8,128)(2,1)S(1)}, bf16[16,32,256]{2,1,0:T(8,128)(2,1)S(1)}, u32[]{:S(2)}, u32[]{:S(2)}) %collective-permute-start.7) | collective-permute-done | bytes 262176 | tf_op jit(solution)/shard_map/ppermute | solution.py:448
  49.4 0.1 convert_add_fusion
  49.5 1.1 %collective-permute-start.8 = (bf16[8,32,256]{2,1,0:T(8,128)(2,1)S(1)}, bf16[8,32,256]{2,1,0:T(8,128)(2,1)S(1)}, u32[]{:S(2)}, u32[]{:S(2)}) collective-permute-start(bf16[8,32,256]{2,1,0:T(8,128)(2,1)S(1)} %slice.84), channel_id=1, source_target_pairs={{0,1},{1,0},{2,6},{3,7},{4,5},{5,4},{6,2},{7,3},{8,9},{9,8},{10,14... | collective-permute-start | bytes 393224 | tf_op jit(solution)/shard_map/ppermute | solution.py:448
  50.6 5.7 %weight_grads.4 = (bf16[32,64,5120]{2,1,0:T(8,128)(2,1)}, f32[32,5120]{1,0:T(8,128)}) custom-call(bf16[2048,256]{1,0:T(8,128)(2,1)S(1)} %get-tuple-element.84.hid_ref, bf16[256,5120]{1,0:T(8,128)(2,1)S(1)} %get-tuple-element.66.lagged_ref, f32[32,5120]{1,0:T(8,128)S(1)} %copy-done.1, bf16[32,64,5120]{2,1,0:T(8,128)(2,1)S(1)} %copy-done), custom_call_target="tpu_custom_call" | custom-call | flops 2147483648 | bytes 16777216 | tf_op jit(solution)/shard_map/weight_grads/pallas_call | solution.py:258
  56.3 0.0 collective-permute-done.8
  56.4 0.1 collective-permute-start.9
  56.5 3.4 %weight_grads.5 = (bf16[32,64,5120]{2,1,0:T(8,128)(2,1)}, f32[32,5120]{1,0:T(8,128)}) custom-call(bf16[2048,256]{1,0:T(8,128)(2,1)S(1)} %get-tuple-element.84.hid_ref, bf16[256,5120]{1,0:T(8,128)(2,1)S(1)} %get-tuple-element.66.lagged_ref, f32[32,5120]{1,0:T(8,128)S(1)} %copy-done.1, ...), custom_call_target="tpu_custom_call", output_to_operand_aliasing={{0}: (4, {}), {1}: (5, {})} | custom-call | flops 1073741824 | bytes 8388608 | tf_op jit(solution)/shard_map/weight_grads/pallas_call | solution.py:258
  59.9 0.0 collective-permute-done.9
  59.9 1.4 %collective-permute-start.10 = (bf16[2,32,256]{2,1,0:T(8,128)(2,1)S(1)}, bf16[2,32,256]{2,1,0:T(8,128)(2,1)S(1)}, u32[]{:S(2)}, u32[]{:S(2)}) collective-permute-start(bf16[2,32,256]{2,1,0:T(8,128)(2,1)S(1)} %slice.86), channel_id=1, source_target_pairs={{0,8},{1,9},{2,10},{3,11},{4,12},{5,13},{6,14},{7,15},{8,0},{9,1},... | collective-permute-start | bytes 98312 | tf_op jit(solution)/shard_map/ppermute | solution.py:448
  61.3 3.4 %weight_grads.6 = (bf16[32,64,5120]{2,1,0:T(8,128)(2,1)}, f32[32,5120]{1,0:T(8,128)}) custom-call(bf16[2048,256]{1,0:T(8,128)(2,1)S(1)} %get-tuple-element.84.hid_ref, bf16[256,5120]{1,0:T(8,128)(2,1)S(1)} %get-tuple-element.66.lagged_ref, f32[32,5120]{1,0:T(8,128)S(1)} %copy-done.1, ...), custom_call_target="tpu_custom_call", output_to_operand_aliasing={{0}: (4, {}), {1}: (5, {})} | custom-call | flops 1073741824 | bytes 8388608 | tf_op jit(solution)/shard_map/weight_grads/pallas_call | solution.py:258
  64.7 0.0 collective-permute-done.10
  64.7 2.5 %collective-permute-start.11 = (bf16[1,32,256]{2,1,0:T(8,128)(2,1)S(1)}, bf16[1,32,256]{2,1,0:T(8,128)(2,1)S(1)}, u32[]{:S(2)}, u32[]{:S(2)}) collective-permute-start(bf16[1,32,256]{2,1,0:T(8,128)(2,1)S(1)} %slice.87), channel_id=1, source_target_pairs={{0,16},{1,17},{2,18},{3,19},{4,20},{5,21},{6,22},{7,23},{8,24},{9,... | collective-permute-start | bytes 49160 | tf_op jit(solution)/shard_map/ppermute | solution.py:448
  67.2 1.4 %grad_dec.1 = f32[3,2048]{1,0:T(4,128)} custom-call(s32[1,2048]{1,0:T(1,128)S(1)} %bitcast.15, bf16[96,256]{1,0:T(8,128)(2,1)S(1)} %get-tuple-element.81.win_ref, f32[3,2048]{1,0:T(4,128)S(1)} %copy-done.2, bf16[3,256,2048]{2,1,0:T(8,128)(2,1)S(1)} %bitcast.12), custom_call_target="tpu_custom_call" | custom-call | flops 603979776 | bytes 3145728 | tf_op jit(solution)/shard_map/grad_dec/pallas_call | solution.py:318
  68.6 0.0 collective-permute-done.11
  68.6 5.4 %collective-permute-start.13 = (f32[32,256]{1,0:T(8,128)S(1)}, f32[32,256]{1,0:T(8,128)S(1)}, u32[]{:S(2)}, u32[]{:S(2)}) collective-permute-start(f32[32,256]{1,0:T(8,128)S(1)} %fusion), channel_id=1, source_target_pairs={{1,2},{2,1},{3,4},{4,3},{5,6},{6,5},{7,8},{8,7},{9,10},{10,9},{11,... | collective-permute-start | bytes 98312 | tf_op jit(solution)/shard_map/ppermute | solution.py:337
  74.0 0.2 collective-permute-start.12
  74.2 3.4 %weight_grads.7 = (bf16[32,64,5120]{2,1,0:T(8,128)(2,1)}, f32[32,5120]{1,0:T(8,128)}) custom-call(bf16[2048,256]{1,0:T(8,128)(2,1)S(1)} %get-tuple-element.84.hid_ref, bf16[256,5120]{1,0:T(8,128)(2,1)S(1)} %get-tuple-element.66.lagged_ref, f32[32,5120]{1,0:T(8,128)S(1)} %copy-done.1, ...), custom_call_target="tpu_custom_call", output_to_operand_aliasing={{0}: (4, {}), {1}: (5, {})} | custom-call | flops 1073741824 | bytes 8388608 | tf_op jit(solution)/shard_map/weight_grads/pallas_call | solution.py:258
  77.5 0.0 collective-permute-done.13
  77.5 0.0 collective-permute-done.12
  77.6 1.5 %grad_enc.1 = f32[3,2048]{1,0:T(4,128)} custom-call(s32[1,2048]{1,0:T(1,128)S(1)} %bitcast.16, f32[96,256]{1,0:T(8,128)S(1)} %pad_maximum_fusion.1.grad_ref, bf16[3,256,2048]{2,1,0:T(8,128)(2,1)S(1)} %bitcast.13), custom_call_target="tpu_custom_call" | custom-call | flops 603979776 | bytes 3145728 | tf_op jit(solution)/shard_map/grad_enc/pallas_call | solution.py:318
  (33 shorter events, 0.3 us)
Async XLA Ops:
  0.6 2.2 %copy-start.7 = (s32[2048]{0:T(1024)S(1)}, s32[2048]{0:T(1024)}, u32[]{:S(2)}) copy-start(s32[2048]{0:T(1024)} %param.10) | copy-start | bytes 24580
  0.6 2.2 %copy-start.2 = (f32[3,2048]{1,0:T(4,128)S(1)}, f32[3,2048]{1,0:T(4,128)}, u32[]{:S(2)}) copy-start(f32[3,2048]{1,0:T(4,128)} %dec_ref.3) | copy-start | bytes 73732
  0.7 2.2 %copy-start.3 = (f32[3,2048]{1,0:T(4,128)S(1)}, f32[3,2048]{1,0:T(4,128)}, u32[]{:S(2)}) copy-start(f32[3,2048]{1,0:T(4,128)} %enc_ref.1) | copy-start | bytes 73732
  2.8 11.9 %copy-start = (bf16[32,64,5120]{2,1,0:T(8,128)(2,1)S(1)}, bf16[32,64,5120]{2,1,0:T(8,128)(2,1)}, u32[]{:S(2)}) copy-start(bf16[32,64,5120]{2,1,0:T(8,128)(2,1)} %weight_ref.15) | copy-start | bytes 62914564
  2.8 11.9 %copy-start.1 = (f32[32,5120]{1,0:T(8,128)S(1)}, f32[32,5120]{1,0:T(8,128)}, u32[]{:S(2)}) copy-start(f32[32,5120]{1,0:T(8,128)} %logit_ref.11) | copy-start | bytes 1966084
  4.6 5.0 %collective-permute-start = (f32[32,256]{1,0:T(8,128)S(1)}, f32[32,256]{1,0:T(8,128)S(1)}, u32[]{:S(2)}, u32[]{:S(2)}) collective-permute-start(f32[32,256]{1,0:T(8,128)S(1)} %get-tuple-element.99), channel_id=1, source_target_pairs={{0,1},{1,0},{2,3},{3,2},{4,5},{5,4},{6,7},{7,6},{8,9},{9,8},{10,11... | collective-permute-start | bytes 98312 | tf_op jit(solution)/shard_map/ppermute | solution.py:337
  6.7 5.6 %collective-permute-start.1 = (f32[32,256]{1,0:T(8,128)S(1)}, f32[32,256]{1,0:T(8,128)S(1)}, u32[]{:S(2)}, u32[]{:S(2)}) collective-permute-start(f32[32,256]{1,0:T(8,128)S(1)} %get-tuple-element.100), channel_id=1, source_target_pairs={{1,2},{2,1},{3,4},{4,3},{5,6},{6,5},{7,8},{8,7},{9,10},{10,9},{11,... | collective-permute-start | bytes 98312 | tf_op jit(solution)/shard_map/ppermute | solution.py:337
  12.4 3.6 %collective-permute-start.2 = (bf16[1,32,256]{2,1,0:T(8,128)(2,1)S(1)}, bf16[1,32,256]{2,1,0:T(8,128)(2,1)S(1)}, u32[]{:S(2)}, u32[]{:S(2)}) collective-permute-start(bf16[1,32,256]{2,1,0:T(8,128)(2,1)S(1)} %get-tuple-element.95), channel_id=1, source_target_pairs={{0,16},{1,17},{2,18},{3,19},{4,20},{5,21},{6,22},{7,23},{8,24},{9,... | collective-permute-start | bytes 49160 | tf_op jit(solution)/shard_map/ppermute | solution.py:402
  15.9 3.0 %collective-permute-start.3 = (bf16[2,32,256]{2,1,0:T(8,128)(2,1)S(1)}, bf16[2,32,256]{2,1,0:T(8,128)(2,1)S(1)}, u32[]{:S(2)}, u32[]{:S(2)}) collective-permute-start(bf16[2,32,256]{2,1,0:T(8,128)(2,1)S(1)} %pad_maximum_fusion.3), channel_id=1, source_target_pairs={{0,8},{1,9},{2,10},{3,11},{4,12},{5,13},{6,14},{7,15},{8,0},{9,1},... | collective-permute-start | bytes 98312 | tf_op jit(solution)/shard_map/ppermute | solution.py:402
  19.0 3.3 %collective-permute-start.4 = (bf16[4,32,256]{2,1,0:T(8,128)(2,1)S(1)}, bf16[4,32,256]{2,1,0:T(8,128)(2,1)S(1)}, u32[]{:S(2)}, u32[]{:S(2)}) collective-permute-start(bf16[4,32,256]{2,1,0:T(8,128)(2,1)S(1)} %pad_maximum_fusion.2), channel_id=1, source_target_pairs={{0,4},{1,5},{2,3},{3,2},{4,0},{5,1},{6,7},{7,6},{8,12},{9,13},{10,... | collective-permute-start | bytes 196616 | tf_op jit(solution)/shard_map/ppermute | solution.py:402
  22.3 4.5 %collective-permute-start.5 = (bf16[8,32,256]{2,1,0:T(8,128)(2,1)S(1)}, bf16[8,32,256]{2,1,0:T(8,128)(2,1)S(1)}, u32[]{:S(2)}, u32[]{:S(2)}) collective-permute-start(bf16[8,32,256]{2,1,0:T(8,128)(2,1)S(1)} %pad_maximum_fusion), channel_id=1, source_target_pairs={{0,1},{1,0},{2,6},{3,7},{4,5},{5,4},{6,2},{7,3},{8,9},{9,8},{10,14... | collective-permute-start | bytes 393224 | tf_op jit(solution)/shard_map/ppermute | solution.py:402
  24.1 10.1 %copy-start.4 = (f32[32,64]{1,0:T(8,128)S(1)}, f32[32,64]{1,0:T(8,128)}, u32[]{:S(2)}) copy-start(f32[32,64]{1,0:T(8,128)} %bias_ref.1) | copy-start | bytes 24580
  24.1 10.1 %copy-start.5 = (f32[32,64]{1,0:T(8,128)S(1)}, f32[32,64]{1,0:T(8,128)}, u32[]{:S(2)}) copy-start(f32[32,64]{1,0:T(8,128)} %out_w_ref.1) | copy-start | bytes 24580
  24.1 10.1 %copy-start.6 = (f32[32]{0:T(128)S(1)}, f32[32]{0:T(128)}, u32[]{:S(2)}) copy-start(f32[32]{0:T(128)} %param.17) | copy-start | bytes 388
  26.8 7.3 %collective-permute-start.6 = (bf16[16,32,256]{2,1,0:T(8,128)(2,1)S(1)}, bf16[16,32,256]{2,1,0:T(8,128)(2,1)S(1)}, u32[]{:S(2)}, u32[]{:S(2)}) collective-permute-start(bf16[16,32,256]{2,1,0:T(8,128)(2,1)S(1)} %get-tuple-element.97), channel_id=1, source_target_pairs={{0,2},{1,3},{2,0},{3,1},{4,6},{5,7},{6,4},{7,5},{8,10},{9,11},{10,... | collective-permute-start | bytes 786440 | tf_op jit(solution)/shard_map/ppermute | solution.py:402
  47.8 1.6 %collective-permute-start.7 = (bf16[16,32,256]{2,1,0:T(8,128)(2,1)S(1)}, bf16[16,32,256]{2,1,0:T(8,128)(2,1)S(1)}, u32[]{:S(2)}, u32[]{:S(2)}) collective-permute-start(bf16[16,32,256]{2,1,0:T(8,128)(2,1)S(1)} %slice.83), channel_id=1, source_target_pairs={{0,2},{1,3},{2,0},{3,1},{4,6},{5,7},{6,4},{7,5},{8,10},{9,11},{10,... | collective-permute-start | bytes 786440 | tf_op jit(solution)/shard_map/ppermute | solution.py:448
  49.5 6.9 %collective-permute-start.8 = (bf16[8,32,256]{2,1,0:T(8,128)(2,1)S(1)}, bf16[8,32,256]{2,1,0:T(8,128)(2,1)S(1)}, u32[]{:S(2)}, u32[]{:S(2)}) collective-permute-start(bf16[8,32,256]{2,1,0:T(8,128)(2,1)S(1)} %slice.84), channel_id=1, source_target_pairs={{0,1},{1,0},{2,6},{3,7},{4,5},{5,4},{6,2},{7,3},{8,9},{9,8},{10,14... | collective-permute-start | bytes 393224 | tf_op jit(solution)/shard_map/ppermute | solution.py:448
  56.4 3.5 %collective-permute-start.9 = (bf16[4,32,256]{2,1,0:T(8,128)(2,1)S(1)}, bf16[4,32,256]{2,1,0:T(8,128)(2,1)S(1)}, u32[]{:S(2)}, u32[]{:S(2)}) collective-permute-start(bf16[4,32,256]{2,1,0:T(8,128)(2,1)S(1)} %slice.85), channel_id=1, source_target_pairs={{0,4},{1,5},{2,3},{3,2},{4,0},{5,1},{6,7},{7,6},{8,12},{9,13},{10,... | collective-permute-start | bytes 196616 | tf_op jit(solution)/shard_map/ppermute | solution.py:448
  59.9 4.8 %collective-permute-start.10 = (bf16[2,32,256]{2,1,0:T(8,128)(2,1)S(1)}, bf16[2,32,256]{2,1,0:T(8,128)(2,1)S(1)}, u32[]{:S(2)}, u32[]{:S(2)}) collective-permute-start(bf16[2,32,256]{2,1,0:T(8,128)(2,1)S(1)} %slice.86), channel_id=1, source_target_pairs={{0,8},{1,9},{2,10},{3,11},{4,12},{5,13},{6,14},{7,15},{8,0},{9,1},... | collective-permute-start | bytes 98312 | tf_op jit(solution)/shard_map/ppermute | solution.py:448
  64.7 3.9 %collective-permute-start.11 = (bf16[1,32,256]{2,1,0:T(8,128)(2,1)S(1)}, bf16[1,32,256]{2,1,0:T(8,128)(2,1)S(1)}, u32[]{:S(2)}, u32[]{:S(2)}) collective-permute-start(bf16[1,32,256]{2,1,0:T(8,128)(2,1)S(1)} %slice.87), channel_id=1, source_target_pairs={{0,16},{1,17},{2,18},{3,19},{4,20},{5,21},{6,22},{7,23},{8,24},{9,... | collective-permute-start | bytes 49160 | tf_op jit(solution)/shard_map/ppermute | solution.py:448
  68.6 8.9 %collective-permute-start.13 = (f32[32,256]{1,0:T(8,128)S(1)}, f32[32,256]{1,0:T(8,128)S(1)}, u32[]{:S(2)}, u32[]{:S(2)}) collective-permute-start(f32[32,256]{1,0:T(8,128)S(1)} %fusion), channel_id=1, source_target_pairs={{1,2},{2,1},{3,4},{4,3},{5,6},{6,5},{7,8},{8,7},{9,10},{10,9},{11,... | collective-permute-start | bytes 98312 | tf_op jit(solution)/shard_map/ppermute | solution.py:337
  74.0 3.6 %collective-permute-start.12 = (f32[32,256]{1,0:T(8,128)S(1)}, f32[32,256]{1,0:T(8,128)S(1)}, u32[]{:S(2)}, u32[]{:S(2)}) collective-permute-start(f32[32,256]{1,0:T(8,128)S(1)} %fusion), channel_id=1, source_target_pairs={{0,1},{1,0},{2,3},{3,2},{4,5},{5,4},{6,7},{7,6},{8,9},{9,8},{10,11... | collective-permute-start | bytes 98312 | tf_op jit(solution)/shard_map/ppermute | solution.py:337

commit v3 on v2

--- a/solution.py
+++ b/solution.py
@@ -43,41 +43,46 @@
     return 8 if lat_dev % 8 == 0 else lat_dev
 
 
-def encode_kernel(loc_ref, enc_ref, dec_ref, fields_ref, enc_out, dec_out, sq_out):
-    width, cells = enc_out.shape[0], loc_ref.shape[1]
-    mask = lax.broadcasted_iota(jnp.int32, (width, cells), 0) == loc_ref[...]
-    total, square = None, None
+def weighted_sums(mask, weight_ref, fields_ref, count):
+    width, total = mask.shape[0], None
     for var in range(fields_ref.shape[0]):
-        dec = dec_ref[var : var + 1, :]
-        weights = [
-            jnp.where(mask, part, 0.0).astype(bf16)
-            for part in pieces(enc_ref[var : var + 1, :], 3) + pieces(dec, 2)
-        ]
-        part = nt_dot(jnp.concatenate(weights, axis=0), fields_ref[var])
-        total = part if total is None else total + part
-        square = dec * dec if square is None else square + dec * dec
-    cut = [total[n * width : (n + 1) * width] for n in range(5)]
-    enc_out[...] = cut[0] + (cut[1] + cut[2])
-    dec_out[...] = cut[3] + cut[4]
+        parts = pieces(weight_ref[var : var + 1, :], count)
+        parts = [jnp.where(mask, part, 0.0).astype(bf16) for part in parts]
+        term = nt_dot(jnp.concatenate(parts, axis=0), fields_ref[var])
+        total = term if total is None else total + term
+    sums = total[(count - 1) * width :]
+    for n in range(count - 2, -1, -1):
+        sums = sums + total[n * width : (n + 1) * width]
+    return sums
+
+
+def encode_kernel(loc_ref, enc_ref, fields_ref, enc_out):
+    enc_out[...] = weighted_sums(mask_of(loc_ref, enc_out.shape[0]), enc_ref, fields_ref, 3)
+
+
+def decode_kernel(loc_ref, dec_ref, fields_ref, dec_out, sq_out):
+    mask = mask_of(loc_ref, dec_out.shape[0])
+    dec_out[...] = weighted_sums(mask, dec_ref, fields_ref, 2)
+    square = jnp.sum(dec_ref[...] * dec_ref[...], axis=0, keepdims=True)
     squares = jnp.sum(jnp.where(mask, square, 0.0), axis=1, keepdims=True)
     sq_out[...] = jnp.broadcast_to(squares, sq_out.shape)
 
 
-def encode(loc, enc_weight, dec_weight, fields3, width):
+def cell_sums(kernel, loc, weight, fields3, width, outs, scale, name):
     var_count, rows, cells = fields3.shape
     return pl.pallas_call(
-        encode_kernel,
-        in_specs=[VMEM] * 4,
-        out_specs=[VMEM] * 3,
-        out_shape=[jax.ShapeDtypeStruct((width, rows), f32)] * 3,
+        kernel,
+        in_specs=[VMEM] * 3,
+        out_specs=[VMEM] * outs,
+        out_shape=[jax.ShapeDtypeStruct((width, rows), f32)] * outs,
         compiler_params=params(12),
         cost_estimate=pl.CostEstimate(
-            flops=50 * width * rows * cells * var_count,
+            flops=scale * width * rows * cells * var_count,
             bytes_accessed=2 * rows * cells * var_count,
             transcendentals=0,
         ),
-        name="encode",
-    )(loc, enc_weight, dec_weight, fields3)
+        name=name,
+    )(loc, weight, fields3)
 
 
 def edge_kernel(group, first, logit_ref, weight_ref, out_ref):
@@ -108,11 +113,14 @@
     return in_vmem(out)
 
 
-def transition_kernel(steps, norm, core, order, inverse, parts, device_ref, lat_ref, own_ref, bias_ref,
+def transition_kernel(steps, norm, core, order, inverse, parts, sources, device_ref, own_ref, bias_ref,
                       out_w_ref, var_ref, dec_ref, sq_ref, *refs):
-    eff = refs[:parts]
-    hid_out, lagged_out, grad_out, direct_out, window_out, lagged, work, hid_t, folded = refs[parts:]
-    blocks, size, rows = lat_ref.shape
+    lat, eff = refs[:sources], refs[sources : sources + parts]
+    outs, scratch = refs[sources + parts : -5], refs[-5:]
+    hid_out, lagged_out, keep_out, send_out, direct_out, window_out = outs
+    lagged, work, hid_t, folded, grad_out = scratch
+    half, size, rows = lat[0].shape
+    blocks = half * sources
     latents = blocks * size
     span, lag_width = eff[0].shape
     lat_dev, hidden = bias_ref.shape
@@ -128,7 +136,7 @@
         return found
 
     for p in range(blocks):
-        values = lat_ref[p].astype(f32)
+        values = lat[p // half][p % half].astype(f32)
         at = pl.multiple_of((device ^ jnp.where(side, order[1][p], order[0][p])) * size, size)
         for lag in range(1, LAGS + 1):
             turned = pltpu.roll(values, lag, 1).astype(bf16)
@@ -175,7 +183,9 @@
         folded[...] = term if lag == 1 else folded[...] + term
     total = folded[...].T
     if blocks == 1:
-        grad_out[0] = total
+        keep_out[0] = total
+        send_out[...] = jnp.zeros_like(send_out)
+        window_out[...] = jnp.zeros_like(window_out)
         return
     for block in range(blocks):
         grad_out[spot(jnp.int32(block))] = total[block * size : (block + 1) * size]
@@ -184,25 +194,32 @@
     above = spot(jnp.minimum(device + 1, blocks - 1))
     for n, at in ((0, below), (1, 0), (2, above)):
         part = slice(n * size, (n + 1) * size)
-        values = lat_ref[at]
-        window_out[part, :] = values
-        grad_out[at] += norm * (values.astype(f32) * sq_ref[part, :] - dec_ref[part, :])
-
-
-def transition(steps, norm, core, order, inverse, device, lat3, own, bias, out_w, var, dec_sums, squares, eff):
-    blocks, size, rows = lat3.shape
+        near, far = (source[at & (half - 1)].astype(f32) for source in lat)
+        values = jnp.where(at >= half, far, near)
+        window_out[part, :] = values.astype(bf16)
+        grad_out[at] += norm * (values * sq_ref[part, :] - dec_ref[part, :])
+    keep_out[...] = grad_out[:half]
+    send_out[...] = grad_out[half:].astype(bf16)
+
+
+def transition(steps, norm, core, order, inverse, device, lat, own, bias, out_w, var, dec_sums, squares, eff):
+    half, size, rows = lat[0].shape
+    blocks = half * len(lat)
     lat_dev, hidden = bias.shape
     span, lag_width = eff[0].shape
     km = lat_dev * hidden
     shape = jax.ShapeDtypeStruct
     return pl.pallas_call(
-        functools.partial(transition_kernel, steps, norm, core, order, inverse, len(eff)),
-        in_specs=[pl.BlockSpec(memory_space=pltpu.SMEM)] + [VMEM] * (7 + len(eff)),
-        out_specs=[VMEM] * 5,
+        functools.partial(
+            transition_kernel, steps, norm, core, order, inverse, len(eff), len(lat)
+        ),
+        in_specs=[pl.BlockSpec(memory_space=pltpu.SMEM)] + [VMEM] * (6 + len(lat) + len(eff)),
+        out_specs=[VMEM] * 6,
         out_shape=[
             shape((km, rows), bf16),
             shape((rows, lag_width), bf16),
-            shape((blocks, size, rows), f32),
+            shape((half, size, rows), f32),
+            shape((half, size, rows) if blocks > 1 else (16, rows), bf16),
             shape((lat_dev, rows), f32),
             shape(dec_sums.shape, bf16),
         ],
@@ -211,15 +228,16 @@
             pltpu.VMEM((2, span, rows), f32),
             pltpu.VMEM((rows, km), bf16),
             pltpu.VMEM((rows, blocks * size), f32),
+            pltpu.VMEM((blocks, size, rows), f32),
         ],
-        compiler_params=params(9),
+        compiler_params=params(8),
         cost_estimate=pl.CostEstimate(
             flops=4 * km * lag_width * rows,
             bytes_accessed=2 * km * lag_width,
             transcendentals=km * rows,
         ),
         name="transition",
-    )(device, lat3, own, bias, out_w, var, dec_sums, squares, *eff)
+    )(device, own, bias, out_w, var, dec_sums, squares, *lat, *eff)
 
 
 def weight_kernel(start, hid_ref, lagged_ref, logit_ref, weight_ref, *refs):
@@ -272,7 +290,7 @@
         ],
         scratch_shapes=[pltpu.VMEM((2, group * hidden, tile), f32)],
         input_output_aliases={4 + n: n for n in range(len(held))},
-        compiler_params=params(16),
+        compiler_params=params(12),
         cost_estimate=pl.CostEstimate(
             flops=2 * km * count * rows, bytes_accessed=4 * km * count, transcendentals=0
         ),
@@ -374,7 +392,11 @@
 
     loc = (cell_latent - (device - 1) * lat_dev)[None]
     fields3 = jnp.transpose(fields.reshape(rows, var_count, cell_count), (1, 0, 2))
-    enc_sums, dec_sums, squares = encode(loc, enc_weight, dec_weight, fields3, width)
+    (enc_sums,) = cell_sums(encode_kernel, loc, enc_weight, fields3, width, 1, 80, "encode")
+    loc_later, _ = lax.optimization_barrier((loc, enc_sums))
+    dec_sums, squares = cell_sums(
+        decode_kernel, loc_later, dec_weight, fields3, width, 2, 50, "decode"
+    )
     first, second, even = from_neighbours(
         enc_sums[:lat_dev], enc_sums[2 * lat_dev :], device, count
     )
@@ -393,14 +415,22 @@
         return value
 
 
+    first, second, dec_sums = lax.optimization_barrier((first, second, dec_sums))
     own = enc_sums[lat_dev : 2 * lat_dev] + first + second
     own_bf = own.astype(bf16)
 
+    def transposed(after):
+        late, _ = lax.optimization_barrier((fields, after))
+        return jnp.transpose(late.reshape(rows, var_count, cell_count), (1, 0, 2))
+
+    fields_late = fields3
     if doubling:
         gathered = own_bf[None]
         for choice in bits:
             got = beside(lax.ppermute(gathered, AXES, swap(choice)), gathered)
-            gathered = jnp.concatenate([gathered, got], axis=0)
+            halves = [gathered, got]
+            if choice != bits[-1]:
+                gathered = jnp.concatenate(halves, axis=0)
         order = [[0], [0]]
         for pair in bits:
             came = order if pair[0] != core else order[::-1]
@@ -417,20 +447,20 @@
         gathered = lax.all_gather(own_bf, AXES, axis=0, tiled=True)
         padded = jnp.pad(gathered, ((lat_dev, lat_dev), (0, 0)))
         window = lax.dynamic_slice_in_dim(padded, device * lat_dev, width, 0)
-        gathered = gathered[None]
+        halves = [gathered[None]]
 
     while len(eff) < parts:
-        gathered = beside(gathered, enc_sums)
+        halves[0] = beside(halves[0], enc_sums)
     eff = [in_vmem(part) for part in eff]
-    hid, lagged, partial, direct, seen = transition(
-        step_count, norm, core, order, inverse, device.astype(jnp.int32)[None], gathered, own,
+    hid, lagged, partial, sent, direct, seen = transition(
+        step_count, norm, core, order, inverse, device.astype(jnp.int32)[None], halves, own,
         hidden_bias, out_weight, noise_var[None], dec_sums, squares, eff,
     )
     window = seen if doubling else window
 
     def decoder(values):
         kernel = functools.partial(grad_dec_kernel, norm)
-        return cell_call(kernel, loc, values, [dec_weight], fields3, "grad_dec")
+        return cell_call(kernel, loc, values, [dec_weight], fields_late, "grad_dec")
 
     if doubling:
         held, total, done = [], partial, 0
@@ -444,8 +474,14 @@
             )
 
         for n, pair in enumerate(reversed(bits)):
-            half = total.shape[0] // 2
-            got = lax.ppermute(total[half:].astype(bf16), AXES, swap(pair))
+            if n == 1:
+                fields_late = transposed(total)
+            if n > 0:
+                half = total.shape[0] // 2
+                total, sent = total[:half], total[half:].astype(bf16)
+            got = lax.ppermute(sent, AXES, swap(pair))
+            if n == 1:
+                got, fields_late = lax.optimization_barrier((got, fields_late))
             if n in shares:
                 held = weight_share(shares[n], held, done)
                 done += shares[n]
@@ -453,7 +489,7 @@
             elif n == 4:
                 seen, _ = lax.optimization_barrier((window, total))
                 got, grad_dec = lax.optimization_barrier((got, decoder(seen)))
-            total = total[:half] + got.astype(f32)
+            total = total + got.astype(f32)
         own_grad = total[0]
         hid, own_grad = lax.optimization_barrier((hid, own_grad))
         first, second, even = from_neighbours(own_grad, own_grad, device, count)
@@ -476,7 +512,7 @@
     grad_window = jnp.concatenate(
         [jnp.where(even, second, first), own_grad, jnp.where(even, first, second)], axis=0
     )
-    grad_enc = cell_call(grad_enc_kernel, loc, grad_window, [], fields3, "grad_enc")
+    grad_enc = cell_call(grad_enc_kernel, loc, grad_window, [], fields_late, "grad_enc")
     return (grad_enc, grad_dec, grad_trans, grad_graph)
 
 

time: 79.5 us -> 78.7 us (0.990)
  waiting for transfers between devices: 8.58 us -> 6.73 us
    ppermute x4, waiting for transfers between devices: 2.73 us -> 0.32 us  [paired(): return lax.ppermute(block, AXES, route)]
    ppermute x4, starting transfers between devices: 10.5 us -> 11.7 us  [paired(): return lax.ppermute(block, AXES, route)]
    ppermute x5, starting transfers between devices: 13.3 us -> 12.3 us  [body(): got = beside(lax.ppermute(gathered, AXES, swap(choice)), gathered)]
    pallas_call x1 -> x2, Pallas kernels: 1.75 us -> 2.32 us  [cell_sums(): pl.pallas_call(kernel, in_specs=[VMEM] * 3, out_specs=[VMEM] * outs, out_...]
    unnamed x21 -> x30, local copies, waits for them, and re-layouts: 2.18 us -> 2.19 us
  transfers between devices with their start and end apart: 14 -> 14, of which waited for: 7 -> 7; matrix products, arithmetic and copies ran while one was open for 0% -> 1% of each run, Pallas kernels for 27% -> 28%
where the time goes in v3:
time: 78.7 us; the launch traced here: 78.5 us
  Pallas kernels  38.4 us (49%)
  starting transfers between devices  29.6 us (38%)
  waiting for transfers between devices  6.73 us (9%)
  local copies, waits for them, and re-layouts  2.64 us (3%)
  between operations  0.98 us (1%)
    pallas_call x4, Pallas kernels, weight_grads(): pl.pallas_call(functools.partial(weight_kernel, first), grid=(count // ti...  15.9 us
    pallas_call x1, Pallas kernels, transition(): pl.pallas_call(functools.partial(transition_kernel, steps, norm, core, or...  13.5 us
    ppermute x5, starting transfers between devices, body(): got = beside(lax.ppermute(gathered, AXES, swap(choice)), gathered)  12.3 us
    ppermute x4, starting transfers between devices, paired(): return lax.ppermute(block, AXES, route)  11.7 us
    ppermute x5, starting transfers between devices, body(): got = lax.ppermute(sent, AXES, swap(pair))  5.57 us
    ppermute x5, waiting for transfers between devices, body(): got = beside(lax.ppermute(gathered, AXES, swap(choice)), gathered)  5.24 us
    pallas_call x4, Pallas kernels, effective(): pl.pallas_call(functools.partial(edge_kernel, group, part * group), in_sp...  3.71 us
    pallas_call x2, Pallas kernels, cell_call(): pl.pallas_call(kernel, in_specs=[VMEM] * (3 + len(extras)), out_specs=VME...  2.87 us
  transfers between devices with their start and end apart: 14, of which 7 were waited for; matrix products, arithmetic and copies ran while one was open for 1% of the time, Pallas kernels for 28%

profile of v3, /device:TPU:1, one launch (start us, length us, event | category | flops | bytes accessed | tf_op | source)
XLA Modules:
  0.0 78.5 jit_solution(16812280160514180240)
XLA Ops:
  0.7 2.1 %copy.19 = bf16[4,64,3,2048]{3,1,0,2:T(8,128)(2,1)S(1)} copy(bf16[4,64,3,2048]{3,1,2,0:T(8,128)(2,1)} %param.9) | data formatting | bytes 6291456 | tf_op args[0]
  2.8 0.0 copy-start.1
  2.8 0.0 slice-start
  2.8 0.0 slice-start.1
  2.8 0.0 slice-start.2
  2.9 0.0 slice-start.3
  2.9 1.1 %encode.1 = f32[96,256]{1,0:T(8,128)S(1)} custom-call(s32[1,2048]{1,0:T(1,128)S(1)} %bitcast.20, f32[3,2048]{1,0:T(4,128)S(1)} %copy-done.2, bf16[3,256,2048]{2,1,0:T(8,128)(2,1)S(1)} %bitcast.18), custom_call_target="tpu_custom_call" | custom-call | flops 12079595520 | bytes 3145728 | tf_op jit(solution)/shard_map/encode/pallas_call | solution.py:73
  4.0 4.8 %collective-permute-start.1 = (f32[32,256]{1,0:T(8,128)S(1)}, f32[32,256]{1,0:T(8,128)S(1)}, u32[]{:S(2)}, u32[]{:S(2)}) collective-permute-start(f32[32,256]{1,0:T(8,128)S(1)} %get-tuple-element.111), channel_id=1, source_target_pairs={{1,2},{2,1},{3,4},{4,3},{5,6},{6,5},{7,8},{8,7},{9,10},{10,9},{11,... | collective-permute-start | bytes 98312 | tf_op jit(solution)/shard_map/ppermute | solution.py:355
  8.8 0.0 slice-start.4
  8.8 0.0 copy-start
  8.8 1.4 %collective-permute-start = (f32[32,256]{1,0:T(8,128)S(1)}, f32[32,256]{1,0:T(8,128)S(1)}, u32[]{:S(2)}, u32[]{:S(2)}) collective-permute-start(f32[32,256]{1,0:T(8,128)S(1)} %get-tuple-element.112), channel_id=1, source_target_pairs={{0,1},{1,0},{2,3},{3,2},{4,5},{5,4},{6,7},{7,6},{8,9},{9,8},{10,11... | collective-permute-start | bytes 98312 | tf_op jit(solution)/shard_map/ppermute | solution.py:355
  10.2 1.2 %decode.1 = (f32[96,256]{1,0:T(8,128)S(1)}, f32[96,256]{1,0:T(8,128)S(1)}) custom-call(s32[1,2048]{1,0:T(1,128)S(1)} %bitcast.21, f32[3,2048]{1,0:T(4,128)S(1)} %copy-done.1, bf16[3,256,2048]{2,1,0:T(8,128)(2,1)S(1)} %bitcast.19), custom_call_target="tpu_custom_call" | custom-call | flops 7549747200 | bytes 3145728 | tf_op jit(solution)/shard_map/decode/pallas_call | solution.py:73
  11.4 0.0 collective-permute-done.1
  11.5 0.3 collective-permute-done
  11.8 2.7 %collective-permute-start.2 = (bf16[1,32,256]{2,1,0:T(8,128)(2,1)S(1)}, bf16[1,32,256]{2,1,0:T(8,128)(2,1)S(1)}, u32[]{:S(2)}, u32[]{:S(2)}) collective-permute-start(bf16[1,32,256]{2,1,0:T(8,128)(2,1)S(1)} %get-tuple-element.109), channel_id=1, source_target_pairs={{0,16},{1,17},{2,18},{3,19},{4,20},{5,21},{6,22},{7,23},{8,24},{9,... | collective-permute-start | bytes 49160 | tf_op jit(solution)/shard_map/ppermute | solution.py:430
  14.5 0.9 %effective.4.refs_2_ = bf16[512,5120]{1,0:T(8,128)(2,1)S(1)} custom-call(f32[32,5120]{1,0:T(8,128)S(1)} %copy-done, bf16[32,64,5120]{2,1,0:T(8,128)(2,1)S(1)} %bitcast.15), custom_call_target="tpu_custom_call" | custom-call | flops 5242880 | bytes 10485760 | tf_op jit(solution)/shard_map/effective/pallas_call | solution.py:100
  15.4 0.2 collective-permute-done.2
  15.6 1.3 %collective-permute-start.3 = (bf16[2,32,256]{2,1,0:T(8,128)(2,1)S(1)}, bf16[2,32,256]{2,1,0:T(8,128)(2,1)S(1)}, u32[]{:S(2)}, u32[]{:S(2)}) collective-permute-start(bf16[2,32,256]{2,1,0:T(8,128)(2,1)S(1)} %pad_maximum_fusion.3), channel_id=1, source_target_pairs={{0,8},{1,9},{2,10},{3,11},{4,12},{5,13},{6,14},{7,15},{8,0},{9,1},... | collective-permute-start | bytes 98312 | tf_op jit(solution)/shard_map/ppermute | solution.py:430
  16.9 0.9 %effective.5.refs_3_ = bf16[512,5120]{1,0:T(8,128)(2,1)S(1)} custom-call(f32[32,5120]{1,0:T(8,128)S(1)} %copy-done, bf16[32,64,5120]{2,1,0:T(8,128)(2,1)S(1)} %bitcast.15), custom_call_target="tpu_custom_call" | custom-call | flops 5242880 | bytes 10485760 | tf_op jit(solution)/shard_map/effective/pallas_call | solution.py:100
  17.9 0.5 collective-permute-done.3
  18.4 1.0 %collective-permute-start.4 = (bf16[4,32,256]{2,1,0:T(8,128)(2,1)S(1)}, bf16[4,32,256]{2,1,0:T(8,128)(2,1)S(1)}, u32[]{:S(2)}, u32[]{:S(2)}) collective-permute-start(bf16[4,32,256]{2,1,0:T(8,128)(2,1)S(1)} %pad_maximum_fusion.2), channel_id=1, source_target_pairs={{0,4},{1,5},{2,3},{3,2},{4,0},{5,1},{6,7},{7,6},{8,12},{9,13},{10,... | collective-permute-start | bytes 196616 | tf_op jit(solution)/shard_map/ppermute | solution.py:430
  19.4 0.9 %effective.6.refs_4_ = bf16[512,5120]{1,0:T(8,128)(2,1)S(1)} custom-call(f32[32,5120]{1,0:T(8,128)S(1)} %copy-done, bf16[32,64,5120]{2,1,0:T(8,128)(2,1)S(1)} %bitcast.15), custom_call_target="tpu_custom_call" | custom-call | flops 5242880 | bytes 10485760 | tf_op jit(solution)/shard_map/effective/pallas_call | solution.py:100
  20.3 1.2 %collective-permute-done.4 = bf16[4,32,256]{2,1,0:T(8,128)(2,1)S(1)} collective-permute-done((bf16[4,32,256]{2,1,0:T(8,128)(2,1)S(1)}, bf16[4,32,256]{2,1,0:T(8,128)(2,1)S(1)}, u32[]{:S(2)}, u32[]{:S(2)}) %collective-permute-start.4) | collective-permute-done | bytes 65568 | tf_op jit(solution)/shard_map/ppermute | solution.py:430
  21.6 1.7 %collective-permute-start.5 = (bf16[8,32,256]{2,1,0:T(8,128)(2,1)S(1)}, bf16[8,32,256]{2,1,0:T(8,128)(2,1)S(1)}, u32[]{:S(2)}, u32[]{:S(2)}) collective-permute-start(bf16[8,32,256]{2,1,0:T(8,128)(2,1)S(1)} %pad_maximum_fusion), channel_id=1, source_target_pairs={{0,1},{1,0},{2,6},{3,7},{4,5},{5,4},{6,2},{7,3},{8,9},{9,8},{10,14... | collective-permute-start | bytes 393224 | tf_op jit(solution)/shard_map/ppermute | solution.py:430
  23.3 0.9 %effective.7.refs_5_ = bf16[512,5120]{1,0:T(8,128)(2,1)S(1)} custom-call(f32[32,5120]{1,0:T(8,128)S(1)} %copy-done, bf16[32,64,5120]{2,1,0:T(8,128)(2,1)S(1)} %bitcast.15), custom_call_target="tpu_custom_call" | custom-call | flops 5242880 | bytes 10485760 | tf_op jit(solution)/shard_map/effective/pallas_call | solution.py:100
  24.3 2.2 %collective-permute-done.5 = bf16[8,32,256]{2,1,0:T(8,128)(2,1)S(1)} collective-permute-done((bf16[8,32,256]{2,1,0:T(8,128)(2,1)S(1)}, bf16[8,32,256]{2,1,0:T(8,128)(2,1)S(1)}, u32[]{:S(2)}, u32[]{:S(2)}) %collective-permute-start.5) | collective-permute-done | bytes 131104 | tf_op jit(solution)/shard_map/ppermute | solution.py:430
  26.5 5.5 %collective-permute-start.6 = (bf16[16,32,256]{2,1,0:T(8,128)(2,1)S(1)}, bf16[16,32,256]{2,1,0:T(8,128)(2,1)S(1)}, u32[]{:S(2)}, u32[]{:S(2)}) collective-permute-start(bf16[16,32,256]{2,1,0:T(8,128)(2,1)S(1)} %constant_dynamic-update-slice_fusion.refs_0_), channel_id=1, source_target_pairs={{0,2},{1,3},{2,0},{3,1},{4,6},{5,7},{6,4},{7,5},{8,10},{9,11},{10,... | collective-permute-start | bytes 786440 | tf_op jit(solution)/shard_map/ppermute | solution.py:430
  32.0 1.2 %collective-permute-done.6.refs_1_ = bf16[16,32,256]{2,1,0:T(8,128)(2,1)S(1)} collective-permute-done((bf16[16,32,256]{2,1,0:T(8,128)(2,1)S(1)}, bf16[16,32,256]{2,1,0:T(8,128)(2,1)S(1)}, u32[]{:S(2)}, u32[]{:S(2)}) %collective-permute-start.6) | collective-permute-done | bytes 262176 | tf_op jit(solution)/shard_map/ppermute | solution.py:430
  33.2 13.5 %transition.1 = (bf16[2048,256]{1,0:T(8,128)(2,1)S(1)}, bf16[256,5120]{1,0:T(8,128)(2,1)S(1)}, f32[16,32,256]{2,1,0:T(8,128)S(1)}, bf16[16,32,256]{2,1,0:T(8,128...) custom-call(s32[1]{0:T(128)} %bitcast.1.device_ref, f32[32,256]{1,0:T(8,128)S(1)} %get-tuple-element.110.own_ref, ...), custom_call_target="tpu_custom_call" | custom-call | flops 10737418240 | bytes 20971520 | tf_op jit(solution)/shard_map/transition/pallas_call | solution.py:212
  46.7 0.4 collective-permute-start.7
  47.1 1.2 %collective-permute-done.7 = bf16[16,32,256]{2,1,0:T(8,128)(2,1)S(1)} collective-permute-done((bf16[16,32,256]{2,1,0:T(8,128)(2,1)S(1)}, bf16[16,32,256]{2,1,0:T(8,128)(2,1)S(1)}, u32[]{:S(2)}, u32[]{:S(2)}) %collective-permute-start.7) | collective-permute-done | bytes 262176 | tf_op jit(solution)/shard_map/ppermute | solution.py:482
  48.3 0.1 convert_add_fusion
  48.4 1.0 %collective-permute-start.8 = (bf16[8,32,256]{2,1,0:T(8,128)(2,1)S(1)}, bf16[8,32,256]{2,1,0:T(8,128)(2,1)S(1)}, u32[]{:S(2)}, u32[]{:S(2)}) collective-permute-start(bf16[8,32,256]{2,1,0:T(8,128)(2,1)S(1)} %slice.74), channel_id=1, source_target_pairs={{0,1},{1,0},{2,6},{3,7},{4,5},{5,4},{6,2},{7,3},{8,9},{9,8},{10,14... | collective-permute-start | bytes 393224 | tf_op jit(solution)/shard_map/ppermute | solution.py:482
  49.4 5.7 %weight_grads.4 = (bf16[32,64,5120]{2,1,0:T(8,128)(2,1)}, f32[32,5120]{1,0:T(8,128)}) custom-call(bf16[2048,256]{1,0:T(8,128)(2,1)S(1)} %get-tuple-element.98.hid_ref, bf16[256,5120]{1,0:T(8,128)(2,1)S(1)} %get-tuple-element.79.lagged_ref, f32[32,5120]{1,0:T(8,128)S(1)} %copy-done, bf16[32,64,5120]{2,1,0:T(8,128)(2,1)S(1)} %bitcast.15), custom_call_target="tpu_custom_call" | custom-call | flops 2147483648 | bytes 16777216 | tf_op jit(solution)/shard_map/weight_grads/pallas_call | solution.py:276
  55.1 0.4 copy.20
  55.5 0.0 collective-permute-done.8
  55.6 0.1 collective-permute-start.9
  55.6 3.4 %weight_grads.5 = (bf16[32,64,5120]{2,1,0:T(8,128)(2,1)}, f32[32,5120]{1,0:T(8,128)}) custom-call(bf16[2048,256]{1,0:T(8,128)(2,1)S(1)} %get-tuple-element.98.hid_ref, bf16[256,5120]{1,0:T(8,128)(2,1)S(1)} %get-tuple-element.79.lagged_ref, f32[32,5120]{1,0:T(8,128)S(1)} %copy-done, ...), custom_call_target="tpu_custom_call", output_to_operand_aliasing={{0}: (4, {}), {1}: (5, {})} | custom-call | flops 1073741824 | bytes 8388608 | tf_op jit(solution)/shard_map/weight_grads/pallas_call | solution.py:276
  59.1 0.0 collective-permute-done.9
  59.1 1.2 %collective-permute-start.10 = (bf16[2,32,256]{2,1,0:T(8,128)(2,1)S(1)}, bf16[2,32,256]{2,1,0:T(8,128)(2,1)S(1)}, u32[]{:S(2)}, u32[]{:S(2)}) collective-permute-start(bf16[2,32,256]{2,1,0:T(8,128)(2,1)S(1)} %slice.76), channel_id=1, source_target_pairs={{0,8},{1,9},{2,10},{3,11},{4,12},{5,13},{6,14},{7,15},{8,0},{9,1},... | collective-permute-start | bytes 98312 | tf_op jit(solution)/shard_map/ppermute | solution.py:482
  60.3 3.4 %weight_grads.6 = (bf16[32,64,5120]{2,1,0:T(8,128)(2,1)}, f32[32,5120]{1,0:T(8,128)}) custom-call(bf16[2048,256]{1,0:T(8,128)(2,1)S(1)} %get-tuple-element.98.hid_ref, bf16[256,5120]{1,0:T(8,128)(2,1)S(1)} %get-tuple-element.79.lagged_ref, f32[32,5120]{1,0:T(8,128)S(1)} %copy-done, ...), custom_call_target="tpu_custom_call", output_to_operand_aliasing={{0}: (4, {}), {1}: (5, {})} | custom-call | flops 1073741824 | bytes 8388608 | tf_op jit(solution)/shard_map/weight_grads/pallas_call | solution.py:276
  63.7 0.0 collective-permute-done.10
  63.7 2.9 %collective-permute-start.11 = (bf16[1,32,256]{2,1,0:T(8,128)(2,1)S(1)}, bf16[1,32,256]{2,1,0:T(8,128)(2,1)S(1)}, u32[]{:S(2)}, u32[]{:S(2)}) collective-permute-start(bf16[1,32,256]{2,1,0:T(8,128)(2,1)S(1)} %slice.77), channel_id=1, source_target_pairs={{0,16},{1,17},{2,18},{3,19},{4,20},{5,21},{6,22},{7,23},{8,24},{9,... | collective-permute-start | bytes 49160 | tf_op jit(solution)/shard_map/ppermute | solution.py:482
  66.6 1.4 %grad_dec.1 = f32[3,2048]{1,0:T(4,128)} custom-call(s32[1,2048]{1,0:T(1,128)S(1)} %bitcast.22, bf16[96,256]{1,0:T(8,128)(2,1)S(1)} %get-tuple-element.94.win_ref, f32[3,2048]{1,0:T(4,128)S(1)} %copy-done.1, bf16[3,256,2048]{2,1,0:T(8,128)(2,1)S(1)} %bitcast.16), custom_call_target="tpu_custom_call" | custom-call | flops 603979776 | bytes 3145728 | tf_op jit(solution)/shard_map/grad_dec/pallas_call | solution.py:336
  68.1 5.0 %collective-permute-start.13 = (f32[32,256]{1,0:T(8,128)S(1)}, f32[32,256]{1,0:T(8,128)S(1)}, u32[]{:S(2)}, u32[]{:S(2)}) collective-permute-start(f32[32,256]{1,0:T(8,128)S(1)} %add_bitcast_fusion), channel_id=1, source_target_pairs={{1,2},{2,1},{3,4},{4,3},{5,6},{6,5},{7,8},{8,7},{9,10},{10,9},{11,... | collective-permute-start | bytes 98312 | tf_op jit(solution)/shard_map/ppermute | solution.py:355
  73.1 0.5 collective-permute-start.12
  73.6 3.4 %weight_grads.7 = (bf16[32,64,5120]{2,1,0:T(8,128)(2,1)}, f32[32,5120]{1,0:T(8,128)}) custom-call(bf16[2048,256]{1,0:T(8,128)(2,1)S(1)} %get-tuple-element.98.hid_ref, bf16[256,5120]{1,0:T(8,128)(2,1)S(1)} %get-tuple-element.79.lagged_ref, f32[32,5120]{1,0:T(8,128)S(1)} %copy-done, ...), custom_call_target="tpu_custom_call", output_to_operand_aliasing={{0}: (4, {}), {1}: (5, {})} | custom-call | flops 1073741824 | bytes 8388608 | tf_op jit(solution)/shard_map/weight_grads/pallas_call | solution.py:276
  77.0 1.5 %grad_enc.1 = f32[3,2048]{1,0:T(4,128)} custom-call(s32[1,2048]{1,0:T(1,128)S(1)} %bitcast.23, f32[96,256]{1,0:T(8,128)S(1)} %pad_maximum_fusion.1.grad_ref, bf16[3,256,2048]{2,1,0:T(8,128)(2,1)S(1)} %bitcast.17), custom_call_target="tpu_custom_call" | custom-call | flops 603979776 | bytes 3145728 | tf_op jit(solution)/shard_map/grad_enc/pallas_call | solution.py:336
  (43 shorter events, 0.2 us)
Async XLA Ops:
  0.6 2.2 %copy-start.7 = (s32[2048]{0:T(1024)S(1)}, s32[2048]{0:T(1024)}, u32[]{:S(2)}) copy-start(s32[2048]{0:T(1024)} %param.10) | copy-start | bytes 24580
  0.6 2.2 %copy-start.2 = (f32[3,2048]{1,0:T(4,128)S(1)}, f32[3,2048]{1,0:T(4,128)}, u32[]{:S(2)}) copy-start(f32[3,2048]{1,0:T(4,128)} %enc_ref.1) | copy-start | bytes 73732
  2.8 7.4 %copy-start.1 = (f32[3,2048]{1,0:T(4,128)S(1)}, f32[3,2048]{1,0:T(4,128)}, u32[]{:S(2)}) copy-start(f32[3,2048]{1,0:T(4,128)} %dec_ref.3) | copy-start | bytes 73732
  2.8 11.6 %slice-start = ((s8[20971520]{0:T(1024)(128)(4,1)}), s8[4194304]{0:T(1024)(128)(4,1)S(1)}, s32[]{:S(2)}) async-start(s8[20971520]{0:T(1024)(128)(4,1)} %bitcast.14), calls=%async_computation | async-start | bytes 8388608
  2.8 11.6 %slice-start.1 = ((s8[20971520]{0:T(1024)(128)(4,1)}), s8[4194304]{0:T(1024)(128)(4,1)S(1)}, s32[]{:S(2)}) async-start(s8[20971520]{0:T(1024)(128)(4,1)} %bitcast.14), calls=%async_computation.1 | async-start | bytes 8388608
  2.8 11.6 %slice-start.2 = ((s8[20971520]{0:T(1024)(128)(4,1)}), s8[4194304]{0:T(1024)(128)(4,1)S(1)}, s32[]{:S(2)}) async-start(s8[20971520]{0:T(1024)(128)(4,1)} %bitcast.14), calls=%async_computation.2 | async-start | bytes 8388608
  2.9 11.6 %slice-start.3 = ((s8[20971520]{0:T(1024)(128)(4,1)}), s8[4194304]{0:T(1024)(128)(4,1)S(1)}, s32[]{:S(2)}) async-start(s8[20971520]{0:T(1024)(128)(4,1)} %bitcast.14), calls=%async_computation.3 | async-start | bytes 8388608
  4.0 7.4 %collective-permute-start.1 = (f32[32,256]{1,0:T(8,128)S(1)}, f32[32,256]{1,0:T(8,128)S(1)}, u32[]{:S(2)}, u32[]{:S(2)}) collective-permute-start(f32[32,256]{1,0:T(8,128)S(1)} %get-tuple-element.111), channel_id=1, source_target_pairs={{1,2},{2,1},{3,4},{4,3},{5,6},{6,5},{7,8},{8,7},{9,10},{10,9},{11,... | collective-permute-start | bytes 98312 | tf_op jit(solution)/shard_map/ppermute | solution.py:355
  8.8 5.7 %slice-start.4 = ((s8[20971520]{0:T(1024)(128)(4,1)}), s8[4194304]{0:T(1024)(128)(4,1)S(1)}, s32[]{:S(2)}) async-start(s8[20971520]{0:T(1024)(128)(4,1)} %bitcast.14), calls=%async_computation.4 | async-start | bytes 8388608
  8.8 5.7 %copy-start = (f32[32,5120]{1,0:T(8,128)S(1)}, f32[32,5120]{1,0:T(8,128)}, u32[]{:S(2)}) copy-start(f32[32,5120]{1,0:T(8,128)} %logit_ref.11) | copy-start | bytes 1966084
  8.8 3.0 %collective-permute-start = (f32[32,256]{1,0:T(8,128)S(1)}, f32[32,256]{1,0:T(8,128)S(1)}, u32[]{:S(2)}, u32[]{:S(2)}) collective-permute-start(f32[32,256]{1,0:T(8,128)S(1)} %get-tuple-element.112), channel_id=1, source_target_pairs={{0,1},{1,0},{2,3},{3,2},{4,5},{5,4},{6,7},{7,6},{8,9},{9,8},{10,11... | collective-permute-start | bytes 98312 | tf_op jit(solution)/shard_map/ppermute | solution.py:355
  11.8 3.8 %collective-permute-start.2 = (bf16[1,32,256]{2,1,0:T(8,128)(2,1)S(1)}, bf16[1,32,256]{2,1,0:T(8,128)(2,1)S(1)}, u32[]{:S(2)}, u32[]{:S(2)}) collective-permute-start(bf16[1,32,256]{2,1,0:T(8,128)(2,1)S(1)} %get-tuple-element.109), channel_id=1, source_target_pairs={{0,16},{1,17},{2,18},{3,19},{4,20},{5,21},{6,22},{7,23},{8,24},{9,... | collective-permute-start | bytes 49160 | tf_op jit(solution)/shard_map/ppermute | solution.py:430
  15.6 2.8 %collective-permute-start.3 = (bf16[2,32,256]{2,1,0:T(8,128)(2,1)S(1)}, bf16[2,32,256]{2,1,0:T(8,128)(2,1)S(1)}, u32[]{:S(2)}, u32[]{:S(2)}) collective-permute-start(bf16[2,32,256]{2,1,0:T(8,128)(2,1)S(1)} %pad_maximum_fusion.3), channel_id=1, source_target_pairs={{0,8},{1,9},{2,10},{3,11},{4,12},{5,13},{6,14},{7,15},{8,0},{9,1},... | collective-permute-start | bytes 98312 | tf_op jit(solution)/shard_map/ppermute | solution.py:430
  18.4 3.2 %collective-permute-start.4 = (bf16[4,32,256]{2,1,0:T(8,128)(2,1)S(1)}, bf16[4,32,256]{2,1,0:T(8,128)(2,1)S(1)}, u32[]{:S(2)}, u32[]{:S(2)}) collective-permute-start(bf16[4,32,256]{2,1,0:T(8,128)(2,1)S(1)} %pad_maximum_fusion.2), channel_id=1, source_target_pairs={{0,4},{1,5},{2,3},{3,2},{4,0},{5,1},{6,7},{7,6},{8,12},{9,13},{10,... | collective-permute-start | bytes 196616 | tf_op jit(solution)/shard_map/ppermute | solution.py:430
  21.6 4.9 %collective-permute-start.5 = (bf16[8,32,256]{2,1,0:T(8,128)(2,1)S(1)}, bf16[8,32,256]{2,1,0:T(8,128)(2,1)S(1)}, u32[]{:S(2)}, u32[]{:S(2)}) collective-permute-start(bf16[8,32,256]{2,1,0:T(8,128)(2,1)S(1)} %pad_maximum_fusion), channel_id=1, source_target_pairs={{0,1},{1,0},{2,6},{3,7},{4,5},{5,4},{6,2},{7,3},{8,9},{9,8},{10,14... | collective-permute-start | bytes 393224 | tf_op jit(solution)/shard_map/ppermute | solution.py:430
  23.3 9.9 %copy-start.3 = (f32[32,64]{1,0:T(8,128)S(1)}, f32[32,64]{1,0:T(8,128)}, u32[]{:S(2)}) copy-start(f32[32,64]{1,0:T(8,128)} %bias_ref.1) | copy-start | bytes 24580
  23.3 9.9 %copy-start.4 = (f32[32,64]{1,0:T(8,128)S(1)}, f32[32,64]{1,0:T(8,128)}, u32[]{:S(2)}) copy-start(f32[32,64]{1,0:T(8,128)} %out_w_ref.1) | copy-start | bytes 24580
  23.3 9.9 %copy-start.5 = (f32[32]{0:T(128)S(1)}, f32[32]{0:T(128)}, u32[]{:S(2)}) copy-start(f32[32]{0:T(128)} %param.17) | copy-start | bytes 388
  26.5 6.7 %collective-permute-start.6 = (bf16[16,32,256]{2,1,0:T(8,128)(2,1)S(1)}, bf16[16,32,256]{2,1,0:T(8,128)(2,1)S(1)}, u32[]{:S(2)}, u32[]{:S(2)}) collective-permute-start(bf16[16,32,256]{2,1,0:T(8,128)(2,1)S(1)} %constant_dynamic-update-slice_fusion.refs_0_), channel_id=1, source_target_pairs={{0,2},{1,3},{2,0},{3,1},{4,6},{5,7},{6,4},{7,5},{8,10},{9,11},{10,... | collective-permute-start | bytes 786440 | tf_op jit(solution)/shard_map/ppermute | solution.py:430
  46.7 1.5 %collective-permute-start.7 = (bf16[16,32,256]{2,1,0:T(8,128)(2,1)S(1)}, bf16[16,32,256]{2,1,0:T(8,128)(2,1)S(1)}, u32[]{:S(2)}, u32[]{:S(2)}) collective-permute-start(bf16[16,32,256]{2,1,0:T(8,128)(2,1)S(1)} %get-tuple-element.76), channel_id=1, source_target_pairs={{0,2},{1,3},{2,0},{3,1},{4,6},{5,7},{6,4},{7,5},{8,10},{9,11},{10,... | collective-permute-start | bytes 786440 | tf_op jit(solution)/shard_map/ppermute | solution.py:482
  48.4 7.2 %collective-permute-start.8 = (bf16[8,32,256]{2,1,0:T(8,128)(2,1)S(1)}, bf16[8,32,256]{2,1,0:T(8,128)(2,1)S(1)}, u32[]{:S(2)}, u32[]{:S(2)}) collective-permute-start(bf16[8,32,256]{2,1,0:T(8,128)(2,1)S(1)} %slice.74), channel_id=1, source_target_pairs={{0,1},{1,0},{2,6},{3,7},{4,5},{5,4},{6,2},{7,3},{8,9},{9,8},{10,14... | collective-permute-start | bytes 393224 | tf_op jit(solution)/shard_map/ppermute | solution.py:482
  49.4 5.7 %copy-start.6 = (bf16[4,64,3,2048]{3,1,2,0:T(8,128)(2,1)S(1)}, bf16[4,64,3,2048]{3,1,2,0:T(8,128)(2,1)}, u32[]{:S(2)}) copy-start(bf16[4,64,3,2048]{3,1,2,0:T(8,128)(2,1)} %param.9) | copy-start | bytes 9437188
  55.6 3.5 %collective-permute-start.9 = (bf16[4,32,256]{2,1,0:T(8,128)(2,1)S(1)}, bf16[4,32,256]{2,1,0:T(8,128)(2,1)S(1)}, u32[]{:S(2)}, u32[]{:S(2)}) collective-permute-start(bf16[4,32,256]{2,1,0:T(8,128)(2,1)S(1)} %slice.75), channel_id=1, source_target_pairs={{0,4},{1,5},{2,3},{3,2},{4,0},{5,1},{6,7},{7,6},{8,12},{9,13},{10,... | collective-permute-start | bytes 196616 | tf_op jit(solution)/shard_map/ppermute | solution.py:482
  59.1 4.6 %collective-permute-start.10 = (bf16[2,32,256]{2,1,0:T(8,128)(2,1)S(1)}, bf16[2,32,256]{2,1,0:T(8,128)(2,1)S(1)}, u32[]{:S(2)}, u32[]{:S(2)}) collective-permute-start(bf16[2,32,256]{2,1,0:T(8,128)(2,1)S(1)} %slice.76), channel_id=1, source_target_pairs={{0,8},{1,9},{2,10},{3,11},{4,12},{5,13},{6,14},{7,15},{8,0},{9,1},... | collective-permute-start | bytes 98312 | tf_op jit(solution)/shard_map/ppermute | solution.py:482
  63.7 4.4 %collective-permute-start.11 = (bf16[1,32,256]{2,1,0:T(8,128)(2,1)S(1)}, bf16[1,32,256]{2,1,0:T(8,128)(2,1)S(1)}, u32[]{:S(2)}, u32[]{:S(2)}) collective-permute-start(bf16[1,32,256]{2,1,0:T(8,128)(2,1)S(1)} %slice.77), channel_id=1, source_target_pairs={{0,16},{1,17},{2,18},{3,19},{4,20},{5,21},{6,22},{7,23},{8,24},{9,... | collective-permute-start | bytes 49160 | tf_op jit(solution)/shard_map/ppermute | solution.py:482
  68.1 8.9 %collective-permute-start.13 = (f32[32,256]{1,0:T(8,128)S(1)}, f32[32,256]{1,0:T(8,128)S(1)}, u32[]{:S(2)}, u32[]{:S(2)}) collective-permute-start(f32[32,256]{1,0:T(8,128)S(1)} %add_bitcast_fusion), channel_id=1, source_target_pairs={{1,2},{2,1},{3,4},{4,3},{5,6},{6,5},{7,8},{8,7},{9,10},{10,9},{11,... | collective-permute-start | bytes 98312 | tf_op jit(solution)/shard_map/ppermute | solution.py:355
  73.1 3.9 %collective-permute-start.12 = (f32[32,256]{1,0:T(8,128)S(1)}, f32[32,256]{1,0:T(8,128)S(1)}, u32[]{:S(2)}, u32[]{:S(2)}) collective-permute-start(f32[32,256]{1,0:T(8,128)S(1)} %add_bitcast_fusion), channel_id=1, source_target_pairs={{0,1},{1,0},{2,3},{3,2},{4,5},{5,4},{6,7},{7,6},{8,9},{9,8},{10,11... | collective-permute-start | bytes 98312 | tf_op jit(solution)/shard_map/ppermute | solution.py:355

commit v4 on v3

--- a/solution.py
+++ b/solution.py
@@ -137,7 +137,10 @@
 
     for p in range(blocks):
         values = lat[p // half][p % half].astype(f32)
-        at = pl.multiple_of((device ^ jnp.where(side, order[1][p], order[0][p])) * size, size)
+        at = 0
+        if blocks > 1:
+            owner = device ^ jnp.where(side, order[1][p], order[0][p])
+            at = pl.multiple_of(owner * size, size)
         for lag in range(1, LAGS + 1):
             turned = pltpu.roll(values, lag, 1).astype(bf16)
             lagged[pl.ds((lag - 1) * latents + at, size), :] = turned

time: 78.7 us -> 78.7 us (level)
  no operation moved by 1% of the time
where the time goes in v4:
time: 78.7 us; the launch traced here: 78.5 us
  Pallas kernels  38.4 us (49%)
  starting transfers between devices  29.6 us (38%)
  waiting for transfers between devices  6.73 us (9%)
  local copies, waits for them, and re-layouts  2.64 us (3%)
  between operations  0.98 us (1%)
    pallas_call x4, Pallas kernels, weight_grads(): pl.pallas_call(functools.partial(weight_kernel, first), grid=(count // ti...  15.9 us
    pallas_call x1, Pallas kernels, transition(): pl.pallas_call(functools.partial(transition_kernel, steps, norm, core, or...  13.5 us
    ppermute x5, starting transfers between devices, body(): got = beside(lax.ppermute(gathered, AXES, swap(choice)), gathered)  12.3 us
    ppermute x4, starting transfers between devices, paired(): return lax.ppermute(block, AXES, route)  11.7 us
    ppermute x5, starting transfers between devices, body(): got = lax.ppermute(sent, AXES, swap(pair))  5.57 us
    ppermute x5, waiting for transfers between devices, body(): got = beside(lax.ppermute(gathered, AXES, swap(choice)), gathered)  5.24 us
    pallas_call x4, Pallas kernels, effective(): pl.pallas_call(functools.partial(edge_kernel, group, part * group), in_sp...  3.71 us
    pallas_call x2, Pallas kernels, cell_call(): pl.pallas_call(kernel, in_specs=[VMEM] * (3 + len(extras)), out_specs=VME...  2.87 us
  transfers between devices with their start and end apart: 14, of which 7 were waited for; matrix products, arithmetic and copies ran while one was open for 1% of the time, Pallas kernels for 28%

profile of v4, /device:TPU:1, one launch (start us, length us, event | category | flops | bytes accessed | tf_op | source)
XLA Modules:
  0.0 78.5 jit_solution(16812280160514180240)
XLA Ops:
  0.7 2.1 %copy.19 = bf16[4,64,3,2048]{3,1,0,2:T(8,128)(2,1)S(1)} copy(bf16[4,64,3,2048]{3,1,2,0:T(8,128)(2,1)} %param.9) | data formatting | bytes 6291456 | tf_op args[0]
  2.8 0.0 copy-start.1
  2.8 0.0 slice-start
  2.8 0.0 slice-start.1
  2.8 0.0 slice-start.2
  2.9 0.0 slice-start.3
  2.9 1.1 %encode.1 = f32[96,256]{1,0:T(8,128)S(1)} custom-call(s32[1,2048]{1,0:T(1,128)S(1)} %bitcast.20, f32[3,2048]{1,0:T(4,128)S(1)} %copy-done.2, bf16[3,256,2048]{2,1,0:T(8,128)(2,1)S(1)} %bitcast.18), custom_call_target="tpu_custom_call" | custom-call | flops 12079595520 | bytes 3145728 | tf_op jit(solution)/shard_map/encode/pallas_call | solution.py:73
  4.0 4.8 %collective-permute-start.1 = (f32[32,256]{1,0:T(8,128)S(1)}, f32[32,256]{1,0:T(8,128)S(1)}, u32[]{:S(2)}, u32[]{:S(2)}) collective-permute-start(f32[32,256]{1,0:T(8,128)S(1)} %get-tuple-element.111), channel_id=1, source_target_pairs={{1,2},{2,1},{3,4},{4,3},{5,6},{6,5},{7,8},{8,7},{9,10},{10,9},{11,... | collective-permute-start | bytes 98312 | tf_op jit(solution)/shard_map/ppermute | solution.py:358
  8.8 0.0 slice-start.4
  8.8 0.0 copy-start
  8.8 1.4 %collective-permute-start = (f32[32,256]{1,0:T(8,128)S(1)}, f32[32,256]{1,0:T(8,128)S(1)}, u32[]{:S(2)}, u32[]{:S(2)}) collective-permute-start(f32[32,256]{1,0:T(8,128)S(1)} %get-tuple-element.112), channel_id=1, source_target_pairs={{0,1},{1,0},{2,3},{3,2},{4,5},{5,4},{6,7},{7,6},{8,9},{9,8},{10,11... | collective-permute-start | bytes 98312 | tf_op jit(solution)/shard_map/ppermute | solution.py:358
  10.2 1.2 %decode.1 = (f32[96,256]{1,0:T(8,128)S(1)}, f32[96,256]{1,0:T(8,128)S(1)}) custom-call(s32[1,2048]{1,0:T(1,128)S(1)} %bitcast.21, f32[3,2048]{1,0:T(4,128)S(1)} %copy-done.1, bf16[3,256,2048]{2,1,0:T(8,128)(2,1)S(1)} %bitcast.19), custom_call_target="tpu_custom_call" | custom-call | flops 7549747200 | bytes 3145728 | tf_op jit(solution)/shard_map/decode/pallas_call | solution.py:73
  11.4 0.0 collective-permute-done.1
  11.5 0.3 collective-permute-done
  11.8 2.7 %collective-permute-start.2 = (bf16[1,32,256]{2,1,0:T(8,128)(2,1)S(1)}, bf16[1,32,256]{2,1,0:T(8,128)(2,1)S(1)}, u32[]{:S(2)}, u32[]{:S(2)}) collective-permute-start(bf16[1,32,256]{2,1,0:T(8,128)(2,1)S(1)} %get-tuple-element.109), channel_id=1, source_target_pairs={{0,16},{1,17},{2,18},{3,19},{4,20},{5,21},{6,22},{7,23},{8,24},{9,... | collective-permute-start | bytes 49160 | tf_op jit(solution)/shard_map/ppermute | solution.py:433
  14.5 0.9 %effective.4.refs_2_ = bf16[512,5120]{1,0:T(8,128)(2,1)S(1)} custom-call(f32[32,5120]{1,0:T(8,128)S(1)} %copy-done, bf16[32,64,5120]{2,1,0:T(8,128)(2,1)S(1)} %bitcast.15), custom_call_target="tpu_custom_call" | custom-call | flops 5242880 | bytes 10485760 | tf_op jit(solution)/shard_map/effective/pallas_call | solution.py:100
  15.4 0.2 collective-permute-done.2
  15.6 1.3 %collective-permute-start.3 = (bf16[2,32,256]{2,1,0:T(8,128)(2,1)S(1)}, bf16[2,32,256]{2,1,0:T(8,128)(2,1)S(1)}, u32[]{:S(2)}, u32[]{:S(2)}) collective-permute-start(bf16[2,32,256]{2,1,0:T(8,128)(2,1)S(1)} %pad_maximum_fusion.3), channel_id=1, source_target_pairs={{0,8},{1,9},{2,10},{3,11},{4,12},{5,13},{6,14},{7,15},{8,0},{9,1},... | collective-permute-start | bytes 98312 | tf_op jit(solution)/shard_map/ppermute | solution.py:433
  16.9 0.9 %effective.5.refs_3_ = bf16[512,5120]{1,0:T(8,128)(2,1)S(1)} custom-call(f32[32,5120]{1,0:T(8,128)S(1)} %copy-done, bf16[32,64,5120]{2,1,0:T(8,128)(2,1)S(1)} %bitcast.15), custom_call_target="tpu_custom_call" | custom-call | flops 5242880 | bytes 10485760 | tf_op jit(solution)/shard_map/effective/pallas_call | solution.py:100
  17.9 0.5 collective-permute-done.3
  18.4 1.0 %collective-permute-start.4 = (bf16[4,32,256]{2,1,0:T(8,128)(2,1)S(1)}, bf16[4,32,256]{2,1,0:T(8,128)(2,1)S(1)}, u32[]{:S(2)}, u32[]{:S(2)}) collective-permute-start(bf16[4,32,256]{2,1,0:T(8,128)(2,1)S(1)} %pad_maximum_fusion.2), channel_id=1, source_target_pairs={{0,4},{1,5},{2,3},{3,2},{4,0},{5,1},{6,7},{7,6},{8,12},{9,13},{10,... | collective-permute-start | bytes 196616 | tf_op jit(solution)/shard_map/ppermute | solution.py:433
  19.4 0.9 %effective.6.refs_4_ = bf16[512,5120]{1,0:T(8,128)(2,1)S(1)} custom-call(f32[32,5120]{1,0:T(8,128)S(1)} %copy-done, bf16[32,64,5120]{2,1,0:T(8,128)(2,1)S(1)} %bitcast.15), custom_call_target="tpu_custom_call" | custom-call | flops 5242880 | bytes 10485760 | tf_op jit(solution)/shard_map/effective/pallas_call | solution.py:100
  20.3 1.2 %collective-permute-done.4 = bf16[4,32,256]{2,1,0:T(8,128)(2,1)S(1)} collective-permute-done((bf16[4,32,256]{2,1,0:T(8,128)(2,1)S(1)}, bf16[4,32,256]{2,1,0:T(8,128)(2,1)S(1)}, u32[]{:S(2)}, u32[]{:S(2)}) %collective-permute-start.4) | collective-permute-done | bytes 65568 | tf_op jit(solution)/shard_map/ppermute | solution.py:433
  21.6 1.7 %collective-permute-start.5 = (bf16[8,32,256]{2,1,0:T(8,128)(2,1)S(1)}, bf16[8,32,256]{2,1,0:T(8,128)(2,1)S(1)}, u32[]{:S(2)}, u32[]{:S(2)}) collective-permute-start(bf16[8,32,256]{2,1,0:T(8,128)(2,1)S(1)} %pad_maximum_fusion), channel_id=1, source_target_pairs={{0,1},{1,0},{2,6},{3,7},{4,5},{5,4},{6,2},{7,3},{8,9},{9,8},{10,14... | collective-permute-start | bytes 393224 | tf_op jit(solution)/shard_map/ppermute | solution.py:433
  23.3 0.9 %effective.7.refs_5_ = bf16[512,5120]{1,0:T(8,128)(2,1)S(1)} custom-call(f32[32,5120]{1,0:T(8,128)S(1)} %copy-done, bf16[32,64,5120]{2,1,0:T(8,128)(2,1)S(1)} %bitcast.15), custom_call_target="tpu_custom_call" | custom-call | flops 5242880 | bytes 10485760 | tf_op jit(solution)/shard_map/effective/pallas_call | solution.py:100
  24.3 2.2 %collective-permute-done.5 = bf16[8,32,256]{2,1,0:T(8,128)(2,1)S(1)} collective-permute-done((bf16[8,32,256]{2,1,0:T(8,128)(2,1)S(1)}, bf16[8,32,256]{2,1,0:T(8,128)(2,1)S(1)}, u32[]{:S(2)}, u32[]{:S(2)}) %collective-permute-start.5) | collective-permute-done | bytes 131104 | tf_op jit(solution)/shard_map/ppermute | solution.py:433
  26.5 5.5 %collective-permute-start.6 = (bf16[16,32,256]{2,1,0:T(8,128)(2,1)S(1)}, bf16[16,32,256]{2,1,0:T(8,128)(2,1)S(1)}, u32[]{:S(2)}, u32[]{:S(2)}) collective-permute-start(bf16[16,32,256]{2,1,0:T(8,128)(2,1)S(1)} %constant_dynamic-update-slice_fusion.refs_0_), channel_id=1, source_target_pairs={{0,2},{1,3},{2,0},{3,1},{4,6},{5,7},{6,4},{7,5},{8,10},{9,11},{10,... | collective-permute-start | bytes 786440 | tf_op jit(solution)/shard_map/ppermute | solution.py:433
  32.0 1.2 %collective-permute-done.6.refs_1_ = bf16[16,32,256]{2,1,0:T(8,128)(2,1)S(1)} collective-permute-done((bf16[16,32,256]{2,1,0:T(8,128)(2,1)S(1)}, bf16[16,32,256]{2,1,0:T(8,128)(2,1)S(1)}, u32[]{:S(2)}, u32[]{:S(2)}) %collective-permute-start.6) | collective-permute-done | bytes 262176 | tf_op jit(solution)/shard_map/ppermute | solution.py:433
  33.2 13.5 %transition.1 = (bf16[2048,256]{1,0:T(8,128)(2,1)S(1)}, bf16[256,5120]{1,0:T(8,128)(2,1)S(1)}, f32[16,32,256]{2,1,0:T(8,128)S(1)}, bf16[16,32,256]{2,1,0:T(8,128...) custom-call(s32[1]{0:T(128)} %bitcast.1.device_ref, f32[32,256]{1,0:T(8,128)S(1)} %get-tuple-element.110.own_ref, ...), custom_call_target="tpu_custom_call" | custom-call | flops 10737418240 | bytes 20971520 | tf_op jit(solution)/shard_map/transition/pallas_call | solution.py:215
  46.7 0.4 collective-permute-start.7
  47.1 1.2 %collective-permute-done.7 = bf16[16,32,256]{2,1,0:T(8,128)(2,1)S(1)} collective-permute-done((bf16[16,32,256]{2,1,0:T(8,128)(2,1)S(1)}, bf16[16,32,256]{2,1,0:T(8,128)(2,1)S(1)}, u32[]{:S(2)}, u32[]{:S(2)}) %collective-permute-start.7) | collective-permute-done | bytes 262176 | tf_op jit(solution)/shard_map/ppermute | solution.py:485
  48.3 0.1 convert_add_fusion
  48.4 1.0 %collective-permute-start.8 = (bf16[8,32,256]{2,1,0:T(8,128)(2,1)S(1)}, bf16[8,32,256]{2,1,0:T(8,128)(2,1)S(1)}, u32[]{:S(2)}, u32[]{:S(2)}) collective-permute-start(bf16[8,32,256]{2,1,0:T(8,128)(2,1)S(1)} %slice.74), channel_id=1, source_target_pairs={{0,1},{1,0},{2,6},{3,7},{4,5},{5,4},{6,2},{7,3},{8,9},{9,8},{10,14... | collective-permute-start | bytes 393224 | tf_op jit(solution)/shard_map/ppermute | solution.py:485
  49.4 5.7 %weight_grads.4 = (bf16[32,64,5120]{2,1,0:T(8,128)(2,1)}, f32[32,5120]{1,0:T(8,128)}) custom-call(bf16[2048,256]{1,0:T(8,128)(2,1)S(1)} %get-tuple-element.98.hid_ref, bf16[256,5120]{1,0:T(8,128)(2,1)S(1)} %get-tuple-element.79.lagged_ref, f32[32,5120]{1,0:T(8,128)S(1)} %copy-done, bf16[32,64,5120]{2,1,0:T(8,128)(2,1)S(1)} %bitcast.15), custom_call_target="tpu_custom_call" | custom-call | flops 2147483648 | bytes 16777216 | tf_op jit(solution)/shard_map/weight_grads/pallas_call | solution.py:279
  55.1 0.4 copy.20
  55.5 0.0 collective-permute-done.8
  55.6 0.1 collective-permute-start.9
  55.6 3.4 %weight_grads.5 = (bf16[32,64,5120]{2,1,0:T(8,128)(2,1)}, f32[32,5120]{1,0:T(8,128)}) custom-call(bf16[2048,256]{1,0:T(8,128)(2,1)S(1)} %get-tuple-element.98.hid_ref, bf16[256,5120]{1,0:T(8,128)(2,1)S(1)} %get-tuple-element.79.lagged_ref, f32[32,5120]{1,0:T(8,128)S(1)} %copy-done, ...), custom_call_target="tpu_custom_call", output_to_operand_aliasing={{0}: (4, {}), {1}: (5, {})} | custom-call | flops 1073741824 | bytes 8388608 | tf_op jit(solution)/shard_map/weight_grads/pallas_call | solution.py:279
  59.1 0.0 collective-permute-done.9
  59.1 1.2 %collective-permute-start.10 = (bf16[2,32,256]{2,1,0:T(8,128)(2,1)S(1)}, bf16[2,32,256]{2,1,0:T(8,128)(2,1)S(1)}, u32[]{:S(2)}, u32[]{:S(2)}) collective-permute-start(bf16[2,32,256]{2,1,0:T(8,128)(2,1)S(1)} %slice.76), channel_id=1, source_target_pairs={{0,8},{1,9},{2,10},{3,11},{4,12},{5,13},{6,14},{7,15},{8,0},{9,1},... | collective-permute-start | bytes 98312 | tf_op jit(solution)/shard_map/ppermute | solution.py:485
  60.3 3.4 %weight_grads.6 = (bf16[32,64,5120]{2,1,0:T(8,128)(2,1)}, f32[32,5120]{1,0:T(8,128)}) custom-call(bf16[2048,256]{1,0:T(8,128)(2,1)S(1)} %get-tuple-element.98.hid_ref, bf16[256,5120]{1,0:T(8,128)(2,1)S(1)} %get-tuple-element.79.lagged_ref, f32[32,5120]{1,0:T(8,128)S(1)} %copy-done, ...), custom_call_target="tpu_custom_call", output_to_operand_aliasing={{0}: (4, {}), {1}: (5, {})} | custom-call | flops 1073741824 | bytes 8388608 | tf_op jit(solution)/shard_map/weight_grads/pallas_call | solution.py:279
  63.7 0.0 collective-permute-done.10
  63.7 2.9 %collective-permute-start.11 = (bf16[1,32,256]{2,1,0:T(8,128)(2,1)S(1)}, bf16[1,32,256]{2,1,0:T(8,128)(2,1)S(1)}, u32[]{:S(2)}, u32[]{:S(2)}) collective-permute-start(bf16[1,32,256]{2,1,0:T(8,128)(2,1)S(1)} %slice.77), channel_id=1, source_target_pairs={{0,16},{1,17},{2,18},{3,19},{4,20},{5,21},{6,22},{7,23},{8,24},{9,... | collective-permute-start | bytes 49160 | tf_op jit(solution)/shard_map/ppermute | solution.py:485
  66.6 1.4 %grad_dec.1 = f32[3,2048]{1,0:T(4,128)} custom-call(s32[1,2048]{1,0:T(1,128)S(1)} %bitcast.22, bf16[96,256]{1,0:T(8,128)(2,1)S(1)} %get-tuple-element.94.win_ref, f32[3,2048]{1,0:T(4,128)S(1)} %copy-done.1, bf16[3,256,2048]{2,1,0:T(8,128)(2,1)S(1)} %bitcast.16), custom_call_target="tpu_custom_call" | custom-call | flops 603979776 | bytes 3145728 | tf_op jit(solution)/shard_map/grad_dec/pallas_call | solution.py:339
  68.1 5.0 %collective-permute-start.13 = (f32[32,256]{1,0:T(8,128)S(1)}, f32[32,256]{1,0:T(8,128)S(1)}, u32[]{:S(2)}, u32[]{:S(2)}) collective-permute-start(f32[32,256]{1,0:T(8,128)S(1)} %add_bitcast_fusion), channel_id=1, source_target_pairs={{1,2},{2,1},{3,4},{4,3},{5,6},{6,5},{7,8},{8,7},{9,10},{10,9},{11,... | collective-permute-start | bytes 98312 | tf_op jit(solution)/shard_map/ppermute | solution.py:358
  73.1 0.5 collective-permute-start.12
  73.6 3.4 %weight_grads.7 = (bf16[32,64,5120]{2,1,0:T(8,128)(2,1)}, f32[32,5120]{1,0:T(8,128)}) custom-call(bf16[2048,256]{1,0:T(8,128)(2,1)S(1)} %get-tuple-element.98.hid_ref, bf16[256,5120]{1,0:T(8,128)(2,1)S(1)} %get-tuple-element.79.lagged_ref, f32[32,5120]{1,0:T(8,128)S(1)} %copy-done, ...), custom_call_target="tpu_custom_call", output_to_operand_aliasing={{0}: (4, {}), {1}: (5, {})} | custom-call | flops 1073741824 | bytes 8388608 | tf_op jit(solution)/shard_map/weight_grads/pallas_call | solution.py:279
  77.0 1.5 %grad_enc.1 = f32[3,2048]{1,0:T(4,128)} custom-call(s32[1,2048]{1,0:T(1,128)S(1)} %bitcast.23, f32[96,256]{1,0:T(8,128)S(1)} %pad_maximum_fusion.1.grad_ref, bf16[3,256,2048]{2,1,0:T(8,128)(2,1)S(1)} %bitcast.17), custom_call_target="tpu_custom_call" | custom-call | flops 603979776 | bytes 3145728 | tf_op jit(solution)/shard_map/grad_enc/pallas_call | solution.py:339
  (43 shorter events, 0.2 us)
Async XLA Ops:
  0.6 2.2 %copy-start.7 = (s32[2048]{0:T(1024)S(1)}, s32[2048]{0:T(1024)}, u32[]{:S(2)}) copy-start(s32[2048]{0:T(1024)} %param.10) | copy-start | bytes 24580
  0.6 2.2 %copy-start.2 = (f32[3,2048]{1,0:T(4,128)S(1)}, f32[3,2048]{1,0:T(4,128)}, u32[]{:S(2)}) copy-start(f32[3,2048]{1,0:T(4,128)} %enc_ref.1) | copy-start | bytes 73732
  2.8 7.4 %copy-start.1 = (f32[3,2048]{1,0:T(4,128)S(1)}, f32[3,2048]{1,0:T(4,128)}, u32[]{:S(2)}) copy-start(f32[3,2048]{1,0:T(4,128)} %dec_ref.3) | copy-start | bytes 73732
  2.8 11.6 %slice-start = ((s8[20971520]{0:T(1024)(128)(4,1)}), s8[4194304]{0:T(1024)(128)(4,1)S(1)}, s32[]{:S(2)}) async-start(s8[20971520]{0:T(1024)(128)(4,1)} %bitcast.14), calls=%async_computation | async-start | bytes 8388608
  2.8 11.6 %slice-start.1 = ((s8[20971520]{0:T(1024)(128)(4,1)}), s8[4194304]{0:T(1024)(128)(4,1)S(1)}, s32[]{:S(2)}) async-start(s8[20971520]{0:T(1024)(128)(4,1)} %bitcast.14), calls=%async_computation.1 | async-start | bytes 8388608
  2.8 11.6 %slice-start.2 = ((s8[20971520]{0:T(1024)(128)(4,1)}), s8[4194304]{0:T(1024)(128)(4,1)S(1)}, s32[]{:S(2)}) async-start(s8[20971520]{0:T(1024)(128)(4,1)} %bitcast.14), calls=%async_computation.2 | async-start | bytes 8388608
  2.9 11.6 %slice-start.3 = ((s8[20971520]{0:T(1024)(128)(4,1)}), s8[4194304]{0:T(1024)(128)(4,1)S(1)}, s32[]{:S(2)}) async-start(s8[20971520]{0:T(1024)(128)(4,1)} %bitcast.14), calls=%async_computation.3 | async-start | bytes 8388608
  4.0 7.4 %collective-permute-start.1 = (f32[32,256]{1,0:T(8,128)S(1)}, f32[32,256]{1,0:T(8,128)S(1)}, u32[]{:S(2)}, u32[]{:S(2)}) collective-permute-start(f32[32,256]{1,0:T(8,128)S(1)} %get-tuple-element.111), channel_id=1, source_target_pairs={{1,2},{2,1},{3,4},{4,3},{5,6},{6,5},{7,8},{8,7},{9,10},{10,9},{11,... | collective-permute-start | bytes 98312 | tf_op jit(solution)/shard_map/ppermute | solution.py:358
  8.8 5.7 %slice-start.4 = ((s8[20971520]{0:T(1024)(128)(4,1)}), s8[4194304]{0:T(1024)(128)(4,1)S(1)}, s32[]{:S(2)}) async-start(s8[20971520]{0:T(1024)(128)(4,1)} %bitcast.14), calls=%async_computation.4 | async-start | bytes 8388608
  8.8 5.7 %copy-start = (f32[32,5120]{1,0:T(8,128)S(1)}, f32[32,5120]{1,0:T(8,128)}, u32[]{:S(2)}) copy-start(f32[32,5120]{1,0:T(8,128)} %logit_ref.11) | copy-start | bytes 1966084
  8.8 3.0 %collective-permute-start = (f32[32,256]{1,0:T(8,128)S(1)}, f32[32,256]{1,0:T(8,128)S(1)}, u32[]{:S(2)}, u32[]{:S(2)}) collective-permute-start(f32[32,256]{1,0:T(8,128)S(1)} %get-tuple-element.112), channel_id=1, source_target_pairs={{0,1},{1,0},{2,3},{3,2},{4,5},{5,4},{6,7},{7,6},{8,9},{9,8},{10,11... | collective-permute-start | bytes 98312 | tf_op jit(solution)/shard_map/ppermute | solution.py:358
  11.8 3.8 %collective-permute-start.2 = (bf16[1,32,256]{2,1,0:T(8,128)(2,1)S(1)}, bf16[1,32,256]{2,1,0:T(8,128)(2,1)S(1)}, u32[]{:S(2)}, u32[]{:S(2)}) collective-permute-start(bf16[1,32,256]{2,1,0:T(8,128)(2,1)S(1)} %get-tuple-element.109), channel_id=1, source_target_pairs={{0,16},{1,17},{2,18},{3,19},{4,20},{5,21},{6,22},{7,23},{8,24},{9,... | collective-permute-start | bytes 49160 | tf_op jit(solution)/shard_map/ppermute | solution.py:433
  15.6 2.8 %collective-permute-start.3 = (bf16[2,32,256]{2,1,0:T(8,128)(2,1)S(1)}, bf16[2,32,256]{2,1,0:T(8,128)(2,1)S(1)}, u32[]{:S(2)}, u32[]{:S(2)}) collective-permute-start(bf16[2,32,256]{2,1,0:T(8,128)(2,1)S(1)} %pad_maximum_fusion.3), channel_id=1, source_target_pairs={{0,8},{1,9},{2,10},{3,11},{4,12},{5,13},{6,14},{7,15},{8,0},{9,1},... | collective-permute-start | bytes 98312 | tf_op jit(solution)/shard_map/ppermute | solution.py:433
  18.4 3.2 %collective-permute-start.4 = (bf16[4,32,256]{2,1,0:T(8,128)(2,1)S(1)}, bf16[4,32,256]{2,1,0:T(8,128)(2,1)S(1)}, u32[]{:S(2)}, u32[]{:S(2)}) collective-permute-start(bf16[4,32,256]{2,1,0:T(8,128)(2,1)S(1)} %pad_maximum_fusion.2), channel_id=1, source_target_pairs={{0,4},{1,5},{2,3},{3,2},{4,0},{5,1},{6,7},{7,6},{8,12},{9,13},{10,... | collective-permute-start | bytes 196616 | tf_op jit(solution)/shard_map/ppermute | solution.py:433
  21.6 4.9 %collective-permute-start.5 = (bf16[8,32,256]{2,1,0:T(8,128)(2,1)S(1)}, bf16[8,32,256]{2,1,0:T(8,128)(2,1)S(1)}, u32[]{:S(2)}, u32[]{:S(2)}) collective-permute-start(bf16[8,32,256]{2,1,0:T(8,128)(2,1)S(1)} %pad_maximum_fusion), channel_id=1, source_target_pairs={{0,1},{1,0},{2,6},{3,7},{4,5},{5,4},{6,2},{7,3},{8,9},{9,8},{10,14... | collective-permute-start | bytes 393224 | tf_op jit(solution)/shard_map/ppermute | solution.py:433
  23.3 9.9 %copy-start.3 = (f32[32,64]{1,0:T(8,128)S(1)}, f32[32,64]{1,0:T(8,128)}, u32[]{:S(2)}) copy-start(f32[32,64]{1,0:T(8,128)} %bias_ref.1) | copy-start | bytes 24580
  23.3 9.9 %copy-start.4 = (f32[32,64]{1,0:T(8,128)S(1)}, f32[32,64]{1,0:T(8,128)}, u32[]{:S(2)}) copy-start(f32[32,64]{1,0:T(8,128)} %out_w_ref.1) | copy-start | bytes 24580
  23.3 9.9 %copy-start.5 = (f32[32]{0:T(128)S(1)}, f32[32]{0:T(128)}, u32[]{:S(2)}) copy-start(f32[32]{0:T(128)} %param.17) | copy-start | bytes 388
  26.5 6.7 %collective-permute-start.6 = (bf16[16,32,256]{2,1,0:T(8,128)(2,1)S(1)}, bf16[16,32,256]{2,1,0:T(8,128)(2,1)S(1)}, u32[]{:S(2)}, u32[]{:S(2)}) collective-permute-start(bf16[16,32,256]{2,1,0:T(8,128)(2,1)S(1)} %constant_dynamic-update-slice_fusion.refs_0_), channel_id=1, source_target_pairs={{0,2},{1,3},{2,0},{3,1},{4,6},{5,7},{6,4},{7,5},{8,10},{9,11},{10,... | collective-permute-start | bytes 786440 | tf_op jit(solution)/shard_map/ppermute | solution.py:433
  46.7 1.5 %collective-permute-start.7 = (bf16[16,32,256]{2,1,0:T(8,128)(2,1)S(1)}, bf16[16,32,256]{2,1,0:T(8,128)(2,1)S(1)}, u32[]{:S(2)}, u32[]{:S(2)}) collective-permute-start(bf16[16,32,256]{2,1,0:T(8,128)(2,1)S(1)} %get-tuple-element.76), channel_id=1, source_target_pairs={{0,2},{1,3},{2,0},{3,1},{4,6},{5,7},{6,4},{7,5},{8,10},{9,11},{10,... | collective-permute-start | bytes 786440 | tf_op jit(solution)/shard_map/ppermute | solution.py:485
  48.4 7.2 %collective-permute-start.8 = (bf16[8,32,256]{2,1,0:T(8,128)(2,1)S(1)}, bf16[8,32,256]{2,1,0:T(8,128)(2,1)S(1)}, u32[]{:S(2)}, u32[]{:S(2)}) collective-permute-start(bf16[8,32,256]{2,1,0:T(8,128)(2,1)S(1)} %slice.74), channel_id=1, source_target_pairs={{0,1},{1,0},{2,6},{3,7},{4,5},{5,4},{6,2},{7,3},{8,9},{9,8},{10,14... | collective-permute-start | bytes 393224 | tf_op jit(solution)/shard_map/ppermute | solution.py:485
  49.4 5.7 %copy-start.6 = (bf16[4,64,3,2048]{3,1,2,0:T(8,128)(2,1)S(1)}, bf16[4,64,3,2048]{3,1,2,0:T(8,128)(2,1)}, u32[]{:S(2)}) copy-start(bf16[4,64,3,2048]{3,1,2,0:T(8,128)(2,1)} %param.9) | copy-start | bytes 9437188
  55.6 3.5 %collective-permute-start.9 = (bf16[4,32,256]{2,1,0:T(8,128)(2,1)S(1)}, bf16[4,32,256]{2,1,0:T(8,128)(2,1)S(1)}, u32[]{:S(2)}, u32[]{:S(2)}) collective-permute-start(bf16[4,32,256]{2,1,0:T(8,128)(2,1)S(1)} %slice.75), channel_id=1, source_target_pairs={{0,4},{1,5},{2,3},{3,2},{4,0},{5,1},{6,7},{7,6},{8,12},{9,13},{10,... | collective-permute-start | bytes 196616 | tf_op jit(solution)/shard_map/ppermute | solution.py:485
  59.1 4.6 %collective-permute-start.10 = (bf16[2,32,256]{2,1,0:T(8,128)(2,1)S(1)}, bf16[2,32,256]{2,1,0:T(8,128)(2,1)S(1)}, u32[]{:S(2)}, u32[]{:S(2)}) collective-permute-start(bf16[2,32,256]{2,1,0:T(8,128)(2,1)S(1)} %slice.76), channel_id=1, source_target_pairs={{0,8},{1,9},{2,10},{3,11},{4,12},{5,13},{6,14},{7,15},{8,0},{9,1},... | collective-permute-start | bytes 98312 | tf_op jit(solution)/shard_map/ppermute | solution.py:485
  63.7 4.4 %collective-permute-start.11 = (bf16[1,32,256]{2,1,0:T(8,128)(2,1)S(1)}, bf16[1,32,256]{2,1,0:T(8,128)(2,1)S(1)}, u32[]{:S(2)}, u32[]{:S(2)}) collective-permute-start(bf16[1,32,256]{2,1,0:T(8,128)(2,1)S(1)} %slice.77), channel_id=1, source_target_pairs={{0,16},{1,17},{2,18},{3,19},{4,20},{5,21},{6,22},{7,23},{8,24},{9,... | collective-permute-start | bytes 49160 | tf_op jit(solution)/shard_map/ppermute | solution.py:485
  68.1 8.9 %collective-permute-start.13 = (f32[32,256]{1,0:T(8,128)S(1)}, f32[32,256]{1,0:T(8,128)S(1)}, u32[]{:S(2)}, u32[]{:S(2)}) collective-permute-start(f32[32,256]{1,0:T(8,128)S(1)} %add_bitcast_fusion), channel_id=1, source_target_pairs={{1,2},{2,1},{3,4},{4,3},{5,6},{6,5},{7,8},{8,7},{9,10},{10,9},{11,... | collective-permute-start | bytes 98312 | tf_op jit(solution)/shard_map/ppermute | solution.py:358
  73.1 3.9 %collective-permute-start.12 = (f32[32,256]{1,0:T(8,128)S(1)}, f32[32,256]{1,0:T(8,128)S(1)}, u32[]{:S(2)}, u32[]{:S(2)}) collective-permute-start(f32[32,256]{1,0:T(8,128)S(1)} %add_bitcast_fusion), channel_id=1, source_target_pairs={{0,1},{1,0},{2,3},{3,2},{4,5},{5,4},{6,7},{7,6},{8,9},{9,8},{10,11... | collective-permute-start | bytes 98312 | tf_op jit(solution)/shard_map/ppermute | solution.py:358
